TPU v7x, 8 devices: a whole 2x2x1 slice. The times are simulated.
8 devices in a mesh: dp: 1 (over z), sp: 8 (over y, x, core).
Axes of the slice: x: 2, y: 2, z: 1, core: 2. Of those that a mesh axis runs over, the one named last changes fastest.
Arguments:
- x: bfloat16 [8, 1024, 256], P('dp', 'sp')
- w_in: bfloat16 [10, 3, 256, 512], replicated
- w_res: bfloat16 [10, 256, 256], replicated
- w_skip: bfloat16 [10, 256, 256], replicated
Outputs:
- output 1: float32 [8, 1024, 256], P('dp', 'sp')
- output 2: float32 [8, 1024, 256], P('dp', 'sp')
All inputs are finite; a program needn't handle non-finite values.
Results may differ from a plain program's by a relative error of at most 0.0046347.
Values are sent between devices in bfloat16 or wider.
A program may use at most 1 GiB of HBM per device.

v0:
```python
import jax
import jax.numpy as jnp
from jax import lax
from jax.sharding import PartitionSpec as P


def neighbour_taps(cur_bf, dilation, n_dev):
    n_rows = cur_bf.shape[1]
    if dilation < n_rows:
        from_prev = lax.ppermute(cur_bf[:, n_rows - dilation:], 'sp', [(src, src + 1) for src in range(n_dev - 1)])
        from_next = lax.ppermute(cur_bf[:, :dilation], 'sp', [(src + 1, src) for src in range(n_dev - 1)])
        left_tap = jnp.concatenate([from_prev, cur_bf[:, :n_rows - dilation]], axis=1)
        right_tap = jnp.concatenate([cur_bf[:, dilation:], from_next], axis=1)
    else:
        n_hops = dilation // n_rows
        left_tap = lax.ppermute(cur_bf, 'sp', [(src, src + n_hops) for src in range(n_dev - n_hops)])
        right_tap = lax.ppermute(cur_bf, 'sp', [(src + n_hops, src) for src in range(n_dev - n_hops)])
    return left_tap, right_tap


def solution(mesh):
    n_dev = mesh.shape['sp']
    act_spec = P('dp', 'sp', None)

    def local_stack(x_local, w_in, w_res, w_skip):
        n_chan = x_local.shape[2]
        residual = x_local.astype(jnp.float32)
        skip_sum = jnp.zeros(x_local.shape[:2] + (w_skip.shape[2],), jnp.float32)
        for layer in range(w_in.shape[0]):
            cur_bf = residual.astype(jnp.bfloat16)
            left_tap, right_tap = neighbour_taps(cur_bf, 2 ** layer, n_dev)
            pre_act = (jnp.einsum('bsc,cf->bsf', left_tap, w_in[layer, 0], preferred_element_type=jnp.float32)
                       + jnp.einsum('bsc,cf->bsf', cur_bf, w_in[layer, 1], preferred_element_type=jnp.float32)
                       + jnp.einsum('bsc,cf->bsf', right_tap, w_in[layer, 2], preferred_element_type=jnp.float32))
            gated = (jnp.tanh(pre_act[..., :n_chan]) * jax.nn.sigmoid(pre_act[..., n_chan:])).astype(jnp.bfloat16)
            residual = residual + jnp.einsum('bsc,cf->bsf', gated, w_res[layer], preferred_element_type=jnp.float32)
            skip_sum = skip_sum + jnp.einsum('bsc,cf->bsf', gated, w_skip[layer], preferred_element_type=jnp.float32)
        return residual, skip_sum

    return jax.shard_map(local_stack, mesh=mesh, in_specs=(act_spec, P(), P(), P()), out_specs=(act_spec, act_spec), check_vma=False)
```

profile of v0, /device:TPU:0, one launch (start us, length us, event | category | flops | bytes accessed | tf_op | source)
XLA Modules:
  0.0 143.0 jit_solution(16535022785831548288)
XLA Ops:
  0.6 0.8 fusion.269
  1.5 2.8 %collective-permute-start = (bf16[8,1,256]{2,1,0:T(2,128)(2,1)S(1)}, bf16[8,1,256]{2,1,0:T(2,128)(2,1)S(1)}, u32[]{:S(2)}, u32[]{:S(2)}) collective-permute-start(bf16[8,1,256]{2,1,0:T(2,128)(2,1)S(1)} %get-tuple-element.27), channel_id=1, source_target_pairs={{0,1},{1,2},{2,3},{3,4},{4,5},{5,6},{6,7}} | collective-permute-start | bytes 12296 | tf_op jit(solution)/shard_map/ppermute | solution.py:10
  4.3 1.3 collective-permute-start.1
  5.6 1.5 %fusion.169 = f32[8,128,512]{2,1,0:T(8,128)S(1)} fusion(bf16[8,128,256]{2,1,0:T(8,128)(2,1)} %param.4, bf16[10,3,256,512]{3,2,1,0:T(8,128)(2,1)} %param.5), kind=kOutput, calls=%fused_computation.198 | convolution fusion | flops 268435456 | bytes 2883584 | tf_op jit(solution)/shard_map/bsc,cf->bsf/dot_general | solution.py:33
  7.3 1.5 %fusion.50 = f32[8,128,512]{2,1,0:T(8,128)S(1)} fusion(bf16[8,127,256]{2,1,0:T(8,128)(2,1)S(1)} %get-tuple-element.25, bf16[8,1,256]{2,1,0:T(2,128)(2,1)S(1)} %collective-permute-done, bf16[10,3,256,512]{3,2,1,0:T(8,128)(2,1)} %param.5), kind=kOutput, calls=%fused_computation.99 | convolution fusion | flops 269484032 | bytes 2883584 | tf_op jit(solution)/shard_map/bsc,cf->bsf/dot_general | solution.py:32
  8.9 0.6 collective-permute-done.1
  9.4 1.5 %add_add_fusion.9 = f32[8,128,512]{2,1,0:T(8,128)S(1)} fusion(f32[8,128,512]{2,1,0:T(8,128)S(1)} %fusion.50, f32[8,128,512]{2,1,0:T(8,128)S(1)} %fusion.169, bf16[8,1,256]{2,1,0:T(2,128)(2,1)S(1)} %collective-permute-done.1, bf16[8,127,256]{2,1,0:T(8,128)(2,1)S(1)} %get-tuple-element.24, bf16[10,3,256,512]{3,2,1,0:T(8,128)(2,1)} %param.5), kind=kOutput, calls=%fused_computation.9 | convolution fusion | flops 270532608 | bytes 7077888 | tf_op jit(solution)/shard_map/bsc,cf->bsf/dot_general | solution.py:34
  11.0 0.4 fusion.40
  11.4 0.9 copy-done.1
  13.1 4.6 %collective-permute-start.2 = (bf16[8,2,256]{2,1,0:T(2,128)(2,1)S(1)}, bf16[8,2,256]{2,1,0:T(2,128)(2,1)S(1)}, u32[]{:S(2)}, u32[]{:S(2)}) collective-permute-start(bf16[8,2,256]{2,1,0:T(2,128)(2,1)S(1)} %get-tuple-element.23), channel_id=1, source_target_pairs={{0,1},{1,2},{2,3},{3,4},{4,5},{5,6},{6,7}} | collective-permute-start | bytes 24584 | tf_op jit(solution)/shard_map/ppermute | solution.py:10
  17.7 1.3 collective-permute-start.3
  19.5 0.4 fusion.60
  19.9 2.1 %collective-permute-done.3 = bf16[8,2,256]{2,1,0:T(2,128)(2,1)S(1)} collective-permute-done((bf16[8,2,256]{2,1,0:T(2,128)(2,1)S(1)}, bf16[8,2,256]{2,1,0:T(2,128)(2,1)S(1)}, u32[]{:S(2)}, u32[]{:S(2)}) %collective-permute-start.3) | collective-permute-done | bytes 8224 | tf_op jit(solution)/shard_map/ppermute | solution.py:11
  22.0 0.4 add_add_fusion.8
  22.4 0.4 fusion.41
  23.6 4.3 %collective-permute-start.4 = (bf16[8,4,256]{2,1,0:T(4,128)(2,1)S(1)}, bf16[8,4,256]{2,1,0:T(4,128)(2,1)S(1)}, u32[]{:S(2)}, u32[]{:S(2)}) collective-permute-start(bf16[8,4,256]{2,1,0:T(4,128)(2,1)S(1)} %get-tuple-element.19), channel_id=1, source_target_pairs={{0,1},{1,2},{2,3},{3,4},{4,5},{5,6},{6,7}} | collective-permute-start | bytes 49160 | tf_op jit(solution)/shard_map/ppermute | solution.py:10
  27.9 1.3 collective-permute-start.5
  29.7 0.4 fusion.70
  30.1 0.9 collective-permute-done.5
  31.0 0.4 add_add_fusion.7
  31.4 0.4 fusion.42
  32.2 0.4 fusion.157
  32.9 5.6 %collective-permute-start.6 = (bf16[8,8,256]{2,1,0:T(8,128)(2,1)S(1)}, bf16[8,8,256]{2,1,0:T(8,128)(2,1)S(1)}, u32[]{:S(2)}, u32[]{:S(2)}) collective-permute-start(bf16[8,8,256]{2,1,0:T(8,128)(2,1)S(1)} %get-tuple-element.15), channel_id=1, source_target_pairs={{0,1},{1,2},{2,3},{3,4},{4,5},{5,6},{6,7}} | collective-permute-start | bytes 98312 | tf_op jit(solution)/shard_map/ppermute | solution.py:10
  38.6 1.3 collective-permute-start.7
  39.9 0.4 fusion.80
  40.3 1.4 collective-permute-done.7
  41.7 0.4 add_add_fusion.6
  42.1 0.4 fusion.43
  42.9 0.4 fusion.153
  43.6 5.0 %collective-permute-start.8 = (bf16[8,16,256]{2,1,0:T(8,128)(2,1)S(1)}, bf16[8,16,256]{2,1,0:T(8,128)(2,1)S(1)}, u32[]{:S(2)}, u32[]{:S(2)}) collective-permute-start(bf16[8,16,256]{2,1,0:T(8,128)(2,1)S(1)} %get-tuple-element.11), channel_id=1, source_target_pairs={{0,1},{1,2},{2,3},{3,4},{4,5},{5,6},{6,7}} | collective-permute-start | bytes 196616 | tf_op jit(solution)/shard_map/ppermute | solution.py:10
  48.7 1.3 collective-permute-start.9
  50.5 1.4 collective-permute-done.9
  51.9 0.4 add_add_fusion.5
  52.3 0.4 fusion.44
  53.1 0.4 fusion.149
  53.8 5.3 %collective-permute-start.10 = (bf16[8,32,256]{2,1,0:T(8,128)(2,1)S(1)}, bf16[8,32,256]{2,1,0:T(8,128)(2,1)S(1)}, u32[]{:S(2)}, u32[]{:S(2)}) collective-permute-start(bf16[8,32,256]{2,1,0:T(8,128)(2,1)S(1)} %get-tuple-element.7), channel_id=1, source_target_pairs={{0,1},{1,2},{2,3},{3,4},{4,5},{5,6},{6,7}} | collective-permute-start | bytes 393224 | tf_op jit(solution)/shard_map/ppermute | solution.py:10
  59.1 1.5 %collective-permute-start.11 = (bf16[8,32,256]{2,1,0:T(8,128)(2,1)S(1)}, bf16[8,32,256]{2,1,0:T(8,128)(2,1)S(1)}, u32[]{:S(2)}, u32[]{:S(2)}) collective-permute-start(bf16[8,32,256]{2,1,0:T(8,128)(2,1)S(1)} %get-tuple-element.6), channel_id=1, source_target_pairs={{1,0},{2,1},{3,2},{4,3},{5,4},{6,5},{7,6}} | collective-permute-start | bytes 393224 | tf_op jit(solution)/shard_map/ppermute | solution.py:11
  61.1 1.2 collective-permute-done.11
  62.8 0.4 fusion.45
  64.0 5.9 %collective-permute-start.12 = (bf16[8,64,256]{2,1,0:T(8,128)(2,1)S(1)}, bf16[8,64,256]{2,1,0:T(8,128)(2,1)S(1)}, u32[]{:S(2)}, u32[]{:S(2)}) collective-permute-start(bf16[8,64,256]{2,1,0:T(8,128)(2,1)S(1)} %get-tuple-element.2), channel_id=1, source_target_pairs={{0,1},{1,2},{2,3},{3,4},{4,5},{5,6},{6,7}} | collective-permute-start | bytes 786440 | tf_op jit(solution)/shard_map/ppermute | solution.py:10
  69.9 1.3 collective-permute-start.13
  71.9 1.4 collective-permute-done.13
  73.7 0.4 fusion.46
  74.5 7.3 %collective-permute-start.14 = (bf16[8,128,256]{2,1,0:T(8,128)(2,1)S(1)}, bf16[8,128,256]{2,1,0:T(8,128)(2,1)S(1)}, u32[]{:S(2)}, u32[]{:S(2)}) collective-permute-start(bf16[8,128,256]{2,1,0:T(8,128)(2,1)S(1)} %get-tuple-element.40), channel_id=1, source_target_pairs={{0,1},{1,2},{2,3},{3,4},{4,5},{5,6},{6,7}} | collective-permute-start | bytes 1572872 | tf_op jit(solution)/shard_map/ppermute | solution.py:16
  81.8 1.3 collective-permute-start.15
  83.1 0.4 fusion.140
  84.3 1.3 collective-permute-done.15
  86.0 0.4 fusion.47
  86.8 12.1 %collective-permute-start.16 = (bf16[8,128,256]{2,1,0:T(8,128)(2,1)S(1)}, bf16[8,128,256]{2,1,0:T(8,128)(2,1)S(1)}, u32[]{:S(2)}, u32[]{:S(2)}) collective-permute-start(bf16[8,128,256]{2,1,0:T(8,128)(2,1)S(1)} %get-tuple-element.42), channel_id=1, source_target_pairs={{0,2},{1,3},{2,4},{3,5},{4,6},{5,7}} | collective-permute-start | bytes 1572872 | tf_op jit(solution)/shard_map/ppermute | solution.py:16
  98.9 1.3 collective-permute-start.17
  100.2 0.4 fusion.132
  100.9 9.8 %collective-permute-done.16 = bf16[8,128,256]{2,1,0:T(8,128)(2,1)S(1)} collective-permute-done((bf16[8,128,256]{2,1,0:T(8,128)(2,1)S(1)}, bf16[8,128,256]{2,1,0:T(8,128)(2,1)S(1)}, u32[]{:S(2)}, u32[]{:S(2)}) %collective-permute-start.16) | collective-permute-done | bytes 524320 | tf_op jit(solution)/shard_map/ppermute | solution.py:16
  111.1 11.6 %collective-permute-done.17 = bf16[8,128,256]{2,1,0:T(8,128)(2,1)S(1)} collective-permute-done((bf16[8,128,256]{2,1,0:T(8,128)(2,1)S(1)}, bf16[8,128,256]{2,1,0:T(8,128)(2,1)S(1)}, u32[]{:S(2)}, u32[]{:S(2)}) %collective-permute-start.17) | collective-permute-done | bytes 524320 | tf_op jit(solution)/shard_map/ppermute | solution.py:17
  122.7 0.4 add_add_fusion.1
  123.1 0.4 fusion.48
  123.9 1.3 collective-permute-start.18
  125.2 1.3 collective-permute-start.19
  126.5 0.4 fusion.124
  127.3 8.2 %collective-permute-done.18 = bf16[8,128,256]{2,1,0:T(8,128)(2,1)S(1)} collective-permute-done((bf16[8,128,256]{2,1,0:T(8,128)(2,1)S(1)}, bf16[8,128,256]{2,1,0:T(8,128)(2,1)S(1)}, u32[]{:S(2)}, u32[]{:S(2)}) %collective-permute-start.18) | collective-permute-done | bytes 524320 | tf_op jit(solution)/shard_map/ppermute | solution.py:16
  135.9 3.7 %collective-permute-done.19 = bf16[8,128,256]{2,1,0:T(8,128)(2,1)S(1)} collective-permute-done((bf16[8,128,256]{2,1,0:T(8,128)(2,1)S(1)}, bf16[8,128,256]{2,1,0:T(8,128)(2,1)S(1)}, u32[]{:S(2)}, u32[]{:S(2)}) %collective-permute-start.19) | collective-permute-done | bytes 524320 | tf_op jit(solution)/shard_map/ppermute | solution.py:17
  139.6 0.4 add_add_fusion
  140.0 0.4 fusion.49
  140.5 1.3 convolution_add_fusion
  141.7 1.3 convolution_add_fusion.9
  (60 shorter events, 11.3 us)
Async XLA Ops:
  0.6 6.5 %copy-start = (bf16[8,128,256]{2,1,0:T(8,128)(2,1)S(1)}, bf16[8,128,256]{2,1,0:T(8,128)(2,1)}, u32[]{:S(2)}) copy-start(bf16[8,128,256]{2,1,0:T(8,128)(2,1)} %param.4) | copy-start | bytes 1572868
  1.5 5.8 %collective-permute-start = (bf16[8,1,256]{2,1,0:T(2,128)(2,1)S(1)}, bf16[8,1,256]{2,1,0:T(2,128)(2,1)S(1)}, u32[]{:S(2)}, u32[]{:S(2)}) collective-permute-start(bf16[8,1,256]{2,1,0:T(2,128)(2,1)S(1)} %get-tuple-element.27), channel_id=1, source_target_pairs={{0,1},{1,2},{2,3},{3,4},{4,5},{5,6},{6,7}} | collective-permute-start | bytes 12296 | tf_op jit(solution)/shard_map/ppermute | solution.py:10
  4.3 5.2 %collective-permute-start.1 = (bf16[8,1,256]{2,1,0:T(2,128)(2,1)S(1)}, bf16[8,1,256]{2,1,0:T(2,128)(2,1)S(1)}, u32[]{:S(2)}, u32[]{:S(2)}) collective-permute-start(bf16[8,1,256]{2,1,0:T(2,128)(2,1)S(1)} %get-tuple-element.26), channel_id=1, source_target_pairs={{1,0},{2,1},{3,2},{4,3},{5,4},{6,5},{7,6}} | collective-permute-start | bytes 12296 | tf_op jit(solution)/shard_map/ppermute | solution.py:11
  7.3 5.3 %slice-start = ((s8[7864320]{0:T(1024)(128)(4,1)}), s8[4194304]{0:T(1024)(128)(4,1)S(1)}, s32[]{:S(2)}) async-start(s8[7864320]{0:T(1024)(128)(4,1)} %bitcast.290), calls=%async_computation | async-start | bytes 8388608
  9.4 3.2 %slice-start.1 = ((s8[7864320]{0:T(1024)(128)(4,1)}), s8[3670016]{0:T(1024)(128)(4,1)S(1)}, s32[]{:S(2)}) async-start(s8[7864320]{0:T(1024)(128)(4,1)} %bitcast.290), calls=%async_computation.1 | async-start | bytes 7340032
  11.0 1.3 copy-start.1
  12.6 6.4 %copy-start.2 = (bf16[10,256,256]{2,1,0:T(8,128)(2,1)S(1)}, bf16[10,256,256]{2,1,0:T(8,128)(2,1)}, u32[]{:S(2)}) copy-start(bf16[10,256,256]{2,1,0:T(8,128)(2,1)} %param.7) | copy-start | bytes 3932164
  13.1 6.4 %collective-permute-start.2 = (bf16[8,2,256]{2,1,0:T(2,128)(2,1)S(1)}, bf16[8,2,256]{2,1,0:T(2,128)(2,1)S(1)}, u32[]{:S(2)}, u32[]{:S(2)}) collective-permute-start(bf16[8,2,256]{2,1,0:T(2,128)(2,1)S(1)} %get-tuple-element.23), channel_id=1, source_target_pairs={{0,1},{1,2},{2,3},{3,4},{4,5},{5,6},{6,7}} | collective-permute-start | bytes 24584 | tf_op jit(solution)/shard_map/ppermute | solution.py:10
  17.7 4.3 %collective-permute-start.3 = (bf16[8,2,256]{2,1,0:T(2,128)(2,1)S(1)}, bf16[8,2,256]{2,1,0:T(2,128)(2,1)S(1)}, u32[]{:S(2)}, u32[]{:S(2)}) collective-permute-start(bf16[8,2,256]{2,1,0:T(2,128)(2,1)S(1)} %get-tuple-element.22), channel_id=1, source_target_pairs={{1,0},{2,1},{3,2},{4,3},{5,4},{6,5},{7,6}} | collective-permute-start | bytes 24584 | tf_op jit(solution)/shard_map/ppermute | solution.py:11
  23.6 6.1 %collective-permute-start.4 = (bf16[8,4,256]{2,1,0:T(4,128)(2,1)S(1)}, bf16[8,4,256]{2,1,0:T(4,128)(2,1)S(1)}, u32[]{:S(2)}, u32[]{:S(2)}) collective-permute-start(bf16[8,4,256]{2,1,0:T(4,128)(2,1)S(1)} %get-tuple-element.19), channel_id=1, source_target_pairs={{0,1},{1,2},{2,3},{3,4},{4,5},{5,6},{6,7}} | collective-permute-start | bytes 49160 | tf_op jit(solution)/shard_map/ppermute | solution.py:10
  27.9 3.1 %collective-permute-start.5 = (bf16[8,4,256]{2,1,0:T(4,128)(2,1)S(1)}, bf16[8,4,256]{2,1,0:T(4,128)(2,1)S(1)}, u32[]{:S(2)}, u32[]{:S(2)}) collective-permute-start(bf16[8,4,256]{2,1,0:T(4,128)(2,1)S(1)} %get-tuple-element.18), channel_id=1, source_target_pairs={{1,0},{2,1},{3,2},{4,3},{5,4},{6,5},{7,6}} | collective-permute-start | bytes 49160 | tf_op jit(solution)/shard_map/ppermute | solution.py:11
  32.9 7.0 %collective-permute-start.6 = (bf16[8,8,256]{2,1,0:T(8,128)(2,1)S(1)}, bf16[8,8,256]{2,1,0:T(8,128)(2,1)S(1)}, u32[]{:S(2)}, u32[]{:S(2)}) collective-permute-start(bf16[8,8,256]{2,1,0:T(8,128)(2,1)S(1)} %get-tuple-element.15), channel_id=1, source_target_pairs={{0,1},{1,2},{2,3},{3,4},{4,5},{5,6},{6,7}} | collective-permute-start | bytes 98312 | tf_op jit(solution)/shard_map/ppermute | solution.py:10
  38.6 3.1 %collective-permute-start.7 = (bf16[8,8,256]{2,1,0:T(8,128)(2,1)S(1)}, bf16[8,8,256]{2,1,0:T(8,128)(2,1)S(1)}, u32[]{:S(2)}, u32[]{:S(2)}) collective-permute-start(bf16[8,8,256]{2,1,0:T(8,128)(2,1)S(1)} %get-tuple-element.14), channel_id=1, source_target_pairs={{1,0},{2,1},{3,2},{4,3},{5,4},{6,5},{7,6}} | collective-permute-start | bytes 98312 | tf_op jit(solution)/shard_map/ppermute | solution.py:11
  43.6 6.4 %collective-permute-start.8 = (bf16[8,16,256]{2,1,0:T(8,128)(2,1)S(1)}, bf16[8,16,256]{2,1,0:T(8,128)(2,1)S(1)}, u32[]{:S(2)}, u32[]{:S(2)}) collective-permute-start(bf16[8,16,256]{2,1,0:T(8,128)(2,1)S(1)} %get-tuple-element.11), channel_id=1, source_target_pairs={{0,1},{1,2},{2,3},{3,4},{4,5},{5,6},{6,7}} | collective-permute-start | bytes 196616 | tf_op jit(solution)/shard_map/ppermute | solution.py:10
  48.7 3.1 %collective-permute-start.9 = (bf16[8,16,256]{2,1,0:T(8,128)(2,1)S(1)}, bf16[8,16,256]{2,1,0:T(8,128)(2,1)S(1)}, u32[]{:S(2)}, u32[]{:S(2)}) collective-permute-start(bf16[8,16,256]{2,1,0:T(8,128)(2,1)S(1)} %get-tuple-element.10), channel_id=1, source_target_pairs={{1,0},{2,1},{3,2},{4,3},{5,4},{6,5},{7,6}} | collective-permute-start | bytes 196616 | tf_op jit(solution)/shard_map/ppermute | solution.py:11
  53.8 6.8 %collective-permute-start.10 = (bf16[8,32,256]{2,1,0:T(8,128)(2,1)S(1)}, bf16[8,32,256]{2,1,0:T(8,128)(2,1)S(1)}, u32[]{:S(2)}, u32[]{:S(2)}) collective-permute-start(bf16[8,32,256]{2,1,0:T(8,128)(2,1)S(1)} %get-tuple-element.7), channel_id=1, source_target_pairs={{0,1},{1,2},{2,3},{3,4},{4,5},{5,6},{6,7}} | collective-permute-start | bytes 393224 | tf_op jit(solution)/shard_map/ppermute | solution.py:10
  59.1 3.2 %collective-permute-start.11 = (bf16[8,32,256]{2,1,0:T(8,128)(2,1)S(1)}, bf16[8,32,256]{2,1,0:T(8,128)(2,1)S(1)}, u32[]{:S(2)}, u32[]{:S(2)}) collective-permute-start(bf16[8,32,256]{2,1,0:T(8,128)(2,1)S(1)} %get-tuple-element.6), channel_id=1, source_target_pairs={{1,0},{2,1},{3,2},{4,3},{5,4},{6,5},{7,6}} | collective-permute-start | bytes 393224 | tf_op jit(solution)/shard_map/ppermute | solution.py:11
  64.0 7.5 %collective-permute-start.12 = (bf16[8,64,256]{2,1,0:T(8,128)(2,1)S(1)}, bf16[8,64,256]{2,1,0:T(8,128)(2,1)S(1)}, u32[]{:S(2)}, u32[]{:S(2)}) collective-permute-start(bf16[8,64,256]{2,1,0:T(8,128)(2,1)S(1)} %get-tuple-element.2), channel_id=1, source_target_pairs={{0,1},{1,2},{2,3},{3,4},{4,5},{5,6},{6,7}} | collective-permute-start | bytes 786440 | tf_op jit(solution)/shard_map/ppermute | solution.py:10
  69.9 3.4 %collective-permute-start.13 = (bf16[8,64,256]{2,1,0:T(8,128)(2,1)S(1)}, bf16[8,64,256]{2,1,0:T(8,128)(2,1)S(1)}, u32[]{:S(2)}, u32[]{:S(2)}) collective-permute-start(bf16[8,64,256]{2,1,0:T(8,128)(2,1)S(1)} %get-tuple-element.3), channel_id=1, source_target_pairs={{1,0},{2,1},{3,2},{4,3},{5,4},{6,5},{7,6}} | collective-permute-start | bytes 786440 | tf_op jit(solution)/shard_map/ppermute | solution.py:11
  74.5 9.4 %collective-permute-start.14 = (bf16[8,128,256]{2,1,0:T(8,128)(2,1)S(1)}, bf16[8,128,256]{2,1,0:T(8,128)(2,1)S(1)}, u32[]{:S(2)}, u32[]{:S(2)}) collective-permute-start(bf16[8,128,256]{2,1,0:T(8,128)(2,1)S(1)} %get-tuple-element.40), channel_id=1, source_target_pairs={{0,1},{1,2},{2,3},{3,4},{4,5},{5,6},{6,7}} | collective-permute-start | bytes 1572872 | tf_op jit(solution)/shard_map/ppermute | solution.py:16
  81.8 3.8 %collective-permute-start.15 = (bf16[8,128,256]{2,1,0:T(8,128)(2,1)S(1)}, bf16[8,128,256]{2,1,0:T(8,128)(2,1)S(1)}, u32[]{:S(2)}, u32[]{:S(2)}) collective-permute-start(bf16[8,128,256]{2,1,0:T(8,128)(2,1)S(1)} %get-tuple-element.40), channel_id=1, source_target_pairs={{1,0},{2,1},{3,2},{4,3},{5,4},{6,5},{7,6}} | collective-permute-start | bytes 1572872 | tf_op jit(solution)/shard_map/ppermute | solution.py:17
  86.8 23.9 %collective-permute-start.16 = (bf16[8,128,256]{2,1,0:T(8,128)(2,1)S(1)}, bf16[8,128,256]{2,1,0:T(8,128)(2,1)S(1)}, u32[]{:S(2)}, u32[]{:S(2)}) collective-permute-start(bf16[8,128,256]{2,1,0:T(8,128)(2,1)S(1)} %get-tuple-element.42), channel_id=1, source_target_pairs={{0,2},{1,3},{2,4},{3,5},{4,6},{5,7}} | collective-permute-start | bytes 1572872 | tf_op jit(solution)/shard_map/ppermute | solution.py:16
  98.9 23.8 %collective-permute-start.17 = (bf16[8,128,256]{2,1,0:T(8,128)(2,1)S(1)}, bf16[8,128,256]{2,1,0:T(8,128)(2,1)S(1)}, u32[]{:S(2)}, u32[]{:S(2)}) collective-permute-start(bf16[8,128,256]{2,1,0:T(8,128)(2,1)S(1)} %get-tuple-element.42), channel_id=1, source_target_pairs={{2,0},{3,1},{4,2},{5,3},{6,4},{7,5}} | collective-permute-start | bytes 1572872 | tf_op jit(solution)/shard_map/ppermute | solution.py:17
  123.9 11.5 %collective-permute-start.18 = (bf16[8,128,256]{2,1,0:T(8,128)(2,1)S(1)}, bf16[8,128,256]{2,1,0:T(8,128)(2,1)S(1)}, u32[]{:S(2)}, u32[]{:S(2)}) collective-permute-start(bf16[8,128,256]{2,1,0:T(8,128)(2,1)S(1)} %get-tuple-element.44), channel_id=1, source_target_pairs={{0,4},{1,5},{2,6},{3,7}} | collective-permute-start | bytes 1572872 | tf_op jit(solution)/shard_map/ppermute | solution.py:16
  125.2 14.4 %collective-permute-start.19 = (bf16[8,128,256]{2,1,0:T(8,128)(2,1)S(1)}, bf16[8,128,256]{2,1,0:T(8,128)(2,1)S(1)}, u32[]{:S(2)}, u32[]{:S(2)}) collective-permute-start(bf16[8,128,256]{2,1,0:T(8,128)(2,1)S(1)} %get-tuple-element.44), channel_id=1, source_target_pairs={{4,0},{5,1},{6,2},{7,3}} | collective-permute-start | bytes 1572872 | tf_op jit(solution)/shard_map/ppermute | solution.py:17
where the time goes:
time: 144 us; the launch traced here: 143 us
  starting transfers between devices  67.2 us (47%)
  waiting for transfers between devices  43.5 us (30%)
  matrix products  24.1 us (17%)
  other arithmetic  4.42 us (3%)
  local copies, waits for them, and re-layouts  2.53 us (2%)
    ppermute x7, starting transfers between devices, neighbour_taps(): lax.ppermute(cur_bf[:, n_rows - dilation:], 'sp', [(src, src + 1) for src...  33.4 us
    ppermute x3, starting transfers between devices, neighbour_taps(): lax.ppermute(cur_bf, 'sp', [(src, src + n_hops) for src in range(n_dev -...  20.7 us
    ppermute x3, waiting for transfers between devices, neighbour_taps(): lax.ppermute(cur_bf, 'sp', [(src, src + n_hops) for src in range(n_dev -...  17.9 us
    ppermute x3, waiting for transfers between devices, neighbour_taps(): lax.ppermute(cur_bf, 'sp', [(src + n_hops, src) for src in range(n_dev -...  16.6 us
    ppermute x7, starting transfers between devices, neighbour_taps(): lax.ppermute(cur_bf[:, :dilation], 'sp', [(src + 1, src) for src in range...  9.23 us
    ppermute x7, waiting for transfers between devices, neighbour_taps(): lax.ppermute(cur_bf[:, :dilation], 'sp', [(src + 1, src) for src in range...  8.9 us
    dot_general x10, matrix products, local_stack(): jnp.einsum('bsc,cf->bsf', cur_bf, w_in[layer, 1], preferred_element_type=...  5.41 us
    dot_general x10, matrix products, local_stack(): jnp.einsum('bsc,cf->bsf', left_tap, w_in[layer, 0], preferred_element_typ...  5.41 us
  transfers between devices with their start and end apart: 20, of which 12 were waited for; matrix products, arithmetic and copies ran while one was open for 7% of the time, Pallas kernels for 0%

commit v1 on v0

v1 whole, which is shorter than its diff:
```python
import functools

import jax
import jax.numpy as jnp
from jax import lax
from jax.experimental import pallas as pl
from jax.experimental.pallas import tpu as pltpu
from jax.sharding import PartitionSpec as P

F32, BF16 = jnp.float32, jnp.bfloat16
MESH = pl.DeviceIdType.MESH
LAYERS = 10
LOCAL = 7
SEQ, BLOCK, CHIP, CHAN = 1024, 128, 256, 256
TILE = 512


def pad_rows(layer):
    return max(2 ** layer, 16)


def flip(index, q):
    out = index
    for bit in range(3):
        if q >> bit & 1:
            out = out + 2 ** bit - 2 ** (bit + 1) * lax.rem(lax.div(index, 2 ** bit), 2)
    return out


def taps(load, d, n):
    centre = load(0, n)
    if d < 16:
        wide = load(-16, n + 32)
        return jnp.concatenate([wide[16 - d:16 - d + n], centre, wide[16 + d:16 + d + n]], axis=1)
    return jnp.concatenate([load(-d, n), centre, load(d, n)], axis=1)


def gated(rows, weight):
    z = jnp.dot(rows, weight, preferred_element_type=F32)
    half = jnp.tanh(z[:, CHAN:] * 0.5)
    return (jnp.tanh(z[:, :CHAN]) * (0.5 + 0.5 * half)).astype(BF16)


def dot(a, b):
    return jnp.dot(a, b, preferred_element_type=F32)


def kernel(x_ref, win_hbm, wres_hbm, wskip_hbm, oh_ref, os_ref, *scratch):
    su = scratch[:LAYERS]
    hu = scratch[LAYERS:LAYERS + LOCAL]
    (win, wres, wskip, hseq, hh, hs, fin_h, fin_s, sa, aland,
     wsem, xsend, xrecv, xloc, psem, hsend, hrecv, asend, arecv, fsem, floc) = scratch[LAYERS + LOCAL:]

    me = lax.axis_index('sp')
    chip, core = lax.div(me, 2), lax.rem(me, 2)
    partner = flip(me, 1)

    def remote(src, dst, send, recv, device):
        return pltpu.make_async_remote_copy(src_ref=src, dst_ref=dst, send_sem=send, recv_sem=recv,
                                            device_id={'sp': device}, device_id_type=MESH)

    weights = []
    for k in range(LAYERS):
        row = [pltpu.make_async_copy(win_hbm.at[k], win.at[k], wsem.at[k, 0]),
               pltpu.make_async_copy(wres_hbm.at[k], wres.at[pl.ds(k * CHAN, CHAN)], wsem.at[k, 1]),
               pltpu.make_async_copy(wskip_hbm.at[k], wskip.at[pl.ds(k * CHAN, CHAN)], wsem.at[k, 2])]
        for copy in row:
            copy.start()
        weights.append(row)

    barrier = pltpu.get_barrier_semaphore()
    for q in range(1, 8):
        pl.semaphore_signal(barrier, inc=1, device_id={'sp': flip(me, q)}, device_id_type=MESH)
    own_rows = pl.ds(pl.multiple_of(16 + BLOCK * me, 16), BLOCK)
    half_rows = pl.ds(pl.multiple_of(16 + BLOCK * core, 16), BLOCK)
    local = [pltpu.make_async_copy(x_ref.at[chip, core], su[0].at[own_rows], xloc.at[0]),
             pltpu.make_async_copy(x_ref.at[:, core], hu[0].at[:, half_rows], xloc.at[1])]
    for copy in local:
        copy.start()
    for k in range(LAYERS):
        pad = pad_rows(k)
        su[k][:pad, :] = jnp.zeros((pad, CHAN), BF16)
        su[k][pad + SEQ:, :] = jnp.zeros((pad, CHAN), BF16)
    pl.semaphore_wait(barrier, 7)

    spread = []
    for q in (6, 7, 2, 4, 3, 5, 1):
        to = flip(me, q)
        copy = remote(x_ref.at[lax.div(to, 2), lax.rem(to, 2)], su[0].at[own_rows], xsend.at[q], xrecv.at[q], to)
        copy.start()
        spread.append(copy)
    mate = remote(x_ref.at[:, 1 - core], hu[0].at[:, half_rows], psem.at[0], psem.at[1], partner)
    mate.start()

    sends = []

    def send_edges(k):
        pad = pad_rows(k)
        for r in range(4):
            there = lax.rem(chip + r, 4)
            for side in range(2):
                src = su[k].at[pl.ds(pl.multiple_of(CHIP * there + side * (CHIP + pad), 16), pad)]
                dst = hu[k].at[chip, pl.ds(side * (CHIP + pad), pad)]
                if r == 0:
                    pltpu.make_async_copy(src, dst, hrecv.at[k, chip, side]).start()
                else:
                    copy = remote(src, dst, hsend.at[k, r, side], hrecv.at[k, chip, side], 2 * there + core)
                    copy.start()
                    sends.append(copy)

    def wait_edges(k):
        pad = pad_rows(k)
        for i in range(4):
            for side in range(2):
                dst = hu[k].at[i, pl.ds(side * (CHIP + pad), pad)]
                pltpu.make_async_copy(dst, dst, hrecv.at[k, i, side]).wait()

    def send_gated(k):
        for q in range(8):
            to = flip(me, q)
            src = sa.at[k - LOCAL, pl.ds(pl.multiple_of(BLOCK * to, BLOCK), BLOCK)]
            dst = aland.at[k - LOCAL, me]
            if q == 0:
                copy = pltpu.make_async_copy(src, dst, arecv.at[k - LOCAL, 0])
            else:
                copy = remote(src, dst, asend.at[k - LOCAL, q], arecv.at[k - LOCAL, q], to)
                sends.append(copy)
            copy.start()

    def wait_gated(k):
        for q in range(8):
            dst = aland.at[k - LOCAL, flip(me, q)]
            pltpu.make_async_copy(dst, dst, arecv.at[k - LOCAL, q]).wait()

    def seq_layer(k):
        d, pad = 2 ** k, pad_rows(k)
        weights[k][0].wait()
        weights[k][1].wait()
        for row in range(0, SEQ, TILE):
            here = pl.ds(row, TILE)
            a = gated(taps(lambda start, size: su[k][pl.ds(row + pad + start, size), :], d, TILE), win[k])
            if k >= LOCAL:
                sa[k - LOCAL, here, :] = a
            if k < LAYERS - 1:
                new = hseq[here, :] + dot(a, wres[pl.ds(k * CHAN, CHAN), :])
                if k < LAYERS - 2:
                    hseq[here, :] = new
                su[k + 1][pl.ds(row + pad_rows(k + 1), TILE), :] = new.astype(BF16)

    def home_layer(k):
        d, pad = 2 ** k, pad_rows(k)
        weights[k][2].wait()
        for i in range(0, 4, 2):
            rows = jnp.concatenate([taps(lambda start, size: hu[k][j, pl.ds(pad + start, size), :], d, CHIP) for j in (i, i + 1)], axis=0)
            a = gated(rows, win[k])
            res = dot(a, wres[pl.ds(k * CHAN, CHAN), :])
            skip = dot(a, wskip[pl.ds(k * CHAN, CHAN), :])
            for j in range(2):
                for half in range(2):
                    cut = slice(j * CHIP + half * BLOCK, j * CHIP + (half + 1) * BLOCK)
                    new = hh[half, i + j] + res[cut]
                    hh[half, i + j] = new
                    hs[half, i + j] = skip[cut] if k == 0 else hs[half, i + j] + skip[cut]
                    if k < LOCAL - 1:
                        hu[k + 1][i + j, pl.ds(pad_rows(k + 1) + half * BLOCK, BLOCK), :] = new.astype(BF16)

    for copy in local:
        copy.wait()
    mate.wait()
    for half in range(2):
        hh[half] = hu[0][:, pl.ds(16 + half * BLOCK, BLOCK), :].astype(F32)
    for copy in spread:
        copy.wait()
    send_edges(0)
    hseq[...] = su[0][pl.ds(16, SEQ), :].astype(F32)
    for k in range(LAYERS):
        seq_layer(k)
        if k + 1 < LOCAL:
            send_edges(k + 1)
        if k >= LOCAL:
            send_gated(k)
    for k in range(LOCAL):
        wait_edges(k)
        home_layer(k)
    moves = []
    for n, (src, dst) in enumerate(((hh, fin_h), (hs, fin_s))):
        move = remote(src.at[1 - core], dst.at[:, core], fsem.at[n, 0], fsem.at[n, 1], partner)
        keep = pltpu.make_async_copy(src.at[core], dst.at[:, core], floc.at[n])
        move.start()
        keep.start()
        moves += [move, keep]
    for k in range(LOCAL, LAYERS):
        weights[k][2].wait()
    for move in moves:
        move.wait()

    def finish(first, last, into_h, into_s):
        a = jnp.concatenate([aland[k - LOCAL].reshape(8 * BLOCK, CHAN) for k in range(first, last)], axis=1)
        span = pl.ds(first * CHAN, (last - first) * CHAN)
        shape = (4, 2, BLOCK, CHAN)
        into_h[...] = fin_h[...] + dot(a, wres[span, :]).reshape(shape)
        into_s[...] = fin_s[...] + dot(a, wskip[span, :]).reshape(shape)

    wait_gated(7)
    wait_gated(8)
    finish(7, 9, fin_h, fin_s)
    wait_gated(9)
    finish(9, 10, oh_ref, os_ref)
    for copy in sends:
        copy.wait_send()


def solution(mesh):
    act_spec = P('dp', 'sp', None)

    def local_stack(x, w_in, w_res, w_skip):
        vmem = lambda shape, dtype: pltpu.VMEM(shape, dtype)
        dma = lambda *shape: pltpu.SemaphoreType.DMA(shape)
        out = jax.ShapeDtypeStruct((4, 2, BLOCK, CHAN), F32)
        scratch = [vmem((SEQ + 2 * pad_rows(k), CHAN), BF16) for k in range(LAYERS)]
        scratch += [vmem((4, CHIP + 2 * pad_rows(k), CHAN), BF16) for k in range(LOCAL)]
        scratch += [vmem((LAYERS, 3 * CHAN, 2 * CHAN), BF16), vmem((LAYERS * CHAN, CHAN), BF16), vmem((LAYERS * CHAN, CHAN), BF16),
                    vmem((SEQ, CHAN), F32), vmem((2, 4, BLOCK, CHAN), F32), vmem((2, 4, BLOCK, CHAN), F32),
                    vmem((4, 2, BLOCK, CHAN), F32), vmem((4, 2, BLOCK, CHAN), F32),
                    vmem((LAYERS - LOCAL, SEQ, CHAN), BF16), vmem((LAYERS - LOCAL, 8, BLOCK, CHAN), BF16)]
        scratch += [dma(LAYERS, 3), dma(8), dma(8), dma(2), dma(2), dma(LOCAL, 4, 2), dma(LOCAL, 4, 2), dma(3, 8), dma(3, 8), dma(2, 2), dma(2)]
        h, s = pl.pallas_call(
            kernel,
            out_shape=(out, out),
            in_specs=[pl.BlockSpec(memory_space=pl.ANY)] * 4,
            out_specs=(pl.BlockSpec(memory_space=pltpu.VMEM),) * 2,
            scratch_shapes=scratch,
            compiler_params=pltpu.CompilerParams(collective_id=0, has_side_effects=True, vmem_limit_bytes=56 * 2 ** 20),
        )(x.reshape(4, 2, BLOCK, CHAN), w_in.reshape(LAYERS, 3 * CHAN, 2 * CHAN), w_res, w_skip)
        return h.reshape(x.shape), s.reshape(x.shape)

    return jax.shard_map(local_stack, mesh=mesh, in_specs=(act_spec, P(), P(), P()), out_specs=(act_spec, act_spec), check_vma=False)
```

time: 144 us -> 48.9 us (0.34)
  starting transfers between devices: 67.2 us -> 0 us
  Pallas kernels: 0 us -> 44.8 us
  waiting for transfers between devices: 43.5 us -> 0 us
  matrix products: 24.1 us -> 0 us
  other arithmetic: 4.42 us -> 0 us
    ppermute x20 -> x0, starting transfers between devices: 67.2 us -> none  [the longest x7 33.4 us: neighbour_taps(): lax.ppermute(cur_bf[:, n_rows - dilation:], 'sp', [(src, src + 1) for src...]
    pallas_call x0 -> x1, Pallas kernels: none -> 44.8 us  [local_stack(): pl.pallas_call(kernel, out_shape=(out, out), in_specs=[pl.BlockSpec(memor...]
    ppermute x20 -> x0, waiting for transfers between devices: 43.5 us -> none  [the longest x3 17.9 us: neighbour_taps(): lax.ppermute(cur_bf, 'sp', [(src, src + n_hops) for src in range(n_dev -...]
    dot_general x50 -> x0, matrix products: 24.1 us -> none  [the longest x10 5.41 us: local_stack(): jnp.einsum('bsc,cf->bsf', cur_bf, w_in[layer, 1], preferred_element_type=...]
    convert_element_type x10 -> x0, other arithmetic: 4.42 us -> none  [local_stack(): (jnp.tanh(pre_act[..., :n_chan]) * jax.nn.sigmoid(pre_act[..., n_chan:]))...]
    unnamed x10 -> x4, local copies, waits for them, and re-layouts: 0.89 us -> 3.33 us
    slice x13 -> x0, local copies, waits for them, and re-layouts: 1.64 us -> none  [the longest x6 0.92 us: neighbour_taps(): cur_bf[:, :dilation]]
  transfers between devices with their start and end apart: 20 -> 0, of which waited for: 12 -> 0; matrix products, arithmetic and copies ran while one was open for 7% -> 0% of each run, Pallas kernels for 0% -> 0%
where the time goes in v1:
time: 48.9 us; the launch traced here: 48.8 us
  Pallas kernels  44.8 us (92%)
  local copies, waits for them, and re-layouts  3.33 us (7%)
  between operations  0.65 us (1%)
    pallas_call x1, Pallas kernels, local_stack(): pl.pallas_call(kernel, out_shape=(out, out), in_specs=[pl.BlockSpec(memor...  44.8 us
    unnamed x4, local copies, waits for them, and re-layouts  3.33 us

profile of v1, /device:TPU:0, one launch (start us, length us, event | category | flops | bytes accessed | tf_op | source)
XLA Modules:
  0.0 48.8 jit_solution(9977612413902478029)
XLA Ops:
  0.6 44.8 %shard_map.59 = (f32[4,2,128,256]{3,2,1,0:T(8,128)}, f32[4,2,128,256]{3,2,1,0:T(8,128)}) custom-call(bf16[4,2,128,256]{3,2,1,0:T(8,128)(2,1)} %bitcast.7, bf16[10,768,512]{2,1,0:T(8,128)(2,1)} %bitcast.4, bf16[10,256,256]{2,1,0:T(8,128)(2,1)} %wres_hbm.1, bf16[10,256,256]{2,1,0:T(8,128)(2,1)} %wskip_hbm.1), custom_call_target="tpu_custom_call" | custom-call | tf_op jit(solution)/shard_map/pallas_call | solution.py:227
  45.5 0.0 copy-start
  45.5 2.4 %copy.8 = f32[8,128,256]{2,1,0:T(8,128)} copy(f32[8,128,256]{2,1,0:T(8,128)} %bitcast.6) | data formatting | bytes 2097152
  47.8 0.0 copy-done
  47.8 1.0 %copy.9 = f32[8,128,256]{2,1,0:T(8,128)} copy(f32[8,128,256]{2,1,0:T(8,128)S(1)} %bitcast.5) | data formatting | bytes 2097152
Async XLA Ops:
  45.5 2.4 %copy-start = (f32[4,2,128,256]{3,2,1,0:T(8,128)S(1)}, f32[4,2,128,256]{3,2,1,0:T(8,128)}, u32[]{:S(2)}) copy-start(f32[4,2,128,256]{3,2,1,0:T(8,128)} %get-tuple-element.5) | copy-start | bytes 3145732

commit v2 on v1

--- a/solution.py
+++ b/solution.py
@@ -10,9 +10,11 @@
 F32, BF16 = jnp.float32, jnp.bfloat16
 MESH = pl.DeviceIdType.MESH
 LAYERS = 10
-LOCAL = 7
+LOCAL = 8
 SEQ, BLOCK, CHIP, CHAN = 1024, 128, 256, 256
 TILE = 512
+STEP = 2
+VMEM_LIMIT = 57 * 2 ** 20
 
 
 def pad_rows(layer):
@@ -45,11 +47,11 @@
     return jnp.dot(a, b, preferred_element_type=F32)
 
 
-def kernel(x_ref, win_hbm, wres_hbm, wskip_hbm, oh_ref, os_ref, *scratch):
+def kernel(x_ref, win_hbm, wres_hbm, wskip_hbm, oh_ref, os_ref, last_ref, *scratch):
     su = scratch[:LAYERS]
     hu = scratch[LAYERS:LAYERS + LOCAL]
     (win, wres, wskip, hseq, hh, hs, fin_h, fin_s, sa, aland,
-     wsem, xsend, xrecv, xloc, psem, hsend, hrecv, asend, arecv, fsem, floc) = scratch[LAYERS + LOCAL:]
+     wsem, xsend, xrecv, xloc, psem, hsend, hrecv, asend, arecv, fsem, floc, osem) = scratch[LAYERS + LOCAL:]
 
     me = lax.axis_index('sp')
     chip, core = lax.div(me, 2), lax.rem(me, 2)
@@ -115,11 +117,14 @@
                 dst = hu[k].at[i, pl.ds(side * (CHIP + pad), pad)]
                 pltpu.make_async_copy(dst, dst, hrecv.at[k, i, side]).wait()
 
+    def landing(k):
+        return last_ref if k == LAYERS - 1 else aland.at[k - LOCAL]
+
     def send_gated(k):
         for q in range(8):
             to = flip(me, q)
             src = sa.at[k - LOCAL, pl.ds(pl.multiple_of(BLOCK * to, BLOCK), BLOCK)]
-            dst = aland.at[k - LOCAL, me]
+            dst = landing(k).at[me]
             if q == 0:
                 copy = pltpu.make_async_copy(src, dst, arecv.at[k - LOCAL, 0])
             else:
@@ -129,7 +134,7 @@
 
     def wait_gated(k):
         for q in range(8):
-            dst = aland.at[k - LOCAL, flip(me, q)]
+            dst = landing(k).at[flip(me, q)]
             pltpu.make_async_copy(dst, dst, arecv.at[k - LOCAL, q]).wait()
 
     def seq_layer(k):
@@ -193,21 +198,26 @@
         weights[k][2].wait()
     for move in moves:
         move.wait()
-
-    def finish(first, last, into_h, into_s):
-        a = jnp.concatenate([aland[k - LOCAL].reshape(8 * BLOCK, CHAN) for k in range(first, last)], axis=1)
-        span = pl.ds(first * CHAN, (last - first) * CHAN)
-        shape = (4, 2, BLOCK, CHAN)
-        into_h[...] = fin_h[...] + dot(a, wres[span, :]).reshape(shape)
-        into_s[...] = fin_s[...] + dot(a, wskip[span, :]).reshape(shape)
-
-    wait_gated(7)
-    wait_gated(8)
-    finish(7, 9, fin_h, fin_s)
-    wait_gated(9)
-    finish(9, 10, oh_ref, os_ref)
+    for k in range(LOCAL, LAYERS - 1):
+        wait_gated(k)
+        span = pl.ds(k * CHAN, CHAN)
+        a = aland[k - LOCAL].reshape(8 * BLOCK, CHAN)
+        fin_h[...] = fin_h[...] + dot(a, wres[span, :]).reshape(fin_h.shape)
+        fin_s[...] = fin_s[...] + dot(a, wskip[span, :]).reshape(fin_s.shape)
+    outs = [pltpu.make_async_copy(fin_h, oh_ref, osem.at[0]), pltpu.make_async_copy(fin_s, os_ref, osem.at[1])]
+    for out in outs:
+        out.start()
+    wait_gated(LAYERS - 1)
+    for out in outs:
+        out.wait()
     for copy in sends:
         copy.wait_send()
+
+
+def last_layer(a_ref, h_ref, s_ref, wres_ref, wskip_ref, oh_ref, os_ref):
+    a = a_ref[...].reshape(-1, CHAN)
+    oh_ref[...] = h_ref[...] + dot(a, wres_ref[0]).reshape(h_ref.shape)
+    os_ref[...] = s_ref[...] + dot(a, wskip_ref[0]).reshape(s_ref.shape)
 
 
 def solution(mesh):
@@ -222,16 +232,24 @@
         scratch += [vmem((LAYERS, 3 * CHAN, 2 * CHAN), BF16), vmem((LAYERS * CHAN, CHAN), BF16), vmem((LAYERS * CHAN, CHAN), BF16),
                     vmem((SEQ, CHAN), F32), vmem((2, 4, BLOCK, CHAN), F32), vmem((2, 4, BLOCK, CHAN), F32),
                     vmem((4, 2, BLOCK, CHAN), F32), vmem((4, 2, BLOCK, CHAN), F32),
-                    vmem((LAYERS - LOCAL, SEQ, CHAN), BF16), vmem((LAYERS - LOCAL, 8, BLOCK, CHAN), BF16)]
-        scratch += [dma(LAYERS, 3), dma(8), dma(8), dma(2), dma(2), dma(LOCAL, 4, 2), dma(LOCAL, 4, 2), dma(3, 8), dma(3, 8), dma(2, 2), dma(2)]
-        h, s = pl.pallas_call(
+                    vmem((LAYERS - LOCAL, SEQ, CHAN), BF16), vmem((LAYERS - LOCAL - 1, 8, BLOCK, CHAN), BF16)]
+        scratch += [dma(LAYERS, 3), dma(8), dma(8), dma(2), dma(2), dma(LOCAL, 4, 2), dma(LOCAL, 4, 2), dma(LAYERS - LOCAL, 8), dma(LAYERS - LOCAL, 8), dma(2, 2), dma(2), dma(2)]
+        h, s, a = pl.pallas_call(
             kernel,
-            out_shape=(out, out),
-            in_specs=[pl.BlockSpec(memory_space=pl.ANY)] * 4,
-            out_specs=(pl.BlockSpec(memory_space=pltpu.VMEM),) * 2,
+            out_shape=(out, out, jax.ShapeDtypeStruct((8, BLOCK, CHAN), BF16)),
+            in_specs=[pl.BlockSpec(memory_space=pltpu.HBM)] * 4,
+            out_specs=(pl.BlockSpec(memory_space=pl.ANY),) * 3,
             scratch_shapes=scratch,
-            compiler_params=pltpu.CompilerParams(collective_id=0, has_side_effects=True, vmem_limit_bytes=56 * 2 ** 20),
+            compiler_params=pltpu.CompilerParams(collective_id=0, has_side_effects=True, vmem_limit_bytes=VMEM_LIMIT),
         )(x.reshape(4, 2, BLOCK, CHAN), w_in.reshape(LAYERS, 3 * CHAN, 2 * CHAN), w_res, w_skip)
-        return h.reshape(x.shape), s.reshape(x.shape)
+        rows = pl.BlockSpec((STEP, BLOCK, CHAN), lambda i: (i, 0, 0))
+        weight = pl.BlockSpec((1, CHAN, CHAN), lambda i: (LAYERS - 1, 0, 0))
+        return pl.pallas_call(
+            last_layer,
+            grid=(8 // STEP,),
+            out_shape=(jax.ShapeDtypeStruct(x.shape, F32),) * 2,
+            in_specs=[rows, rows, rows, weight, weight],
+            out_specs=(rows, rows),
+        )(a, h.reshape(x.shape), s.reshape(x.shape), w_res, w_skip)
 
     return jax.shard_map(local_stack, mesh=mesh, in_specs=(act_spec, P(), P(), P()), out_specs=(act_spec, act_spec), check_vma=False)

time: 48.9 us -> 48.3 us (0.988)
  local copies, waits for them, and re-layouts: 3.33 us -> 0 us
  Pallas kernels: 44.8 us -> 47.5 us
    unnamed x4 -> x0, local copies, waits for them, and re-layouts: 3.33 us -> none
    pallas_call x1 -> x2, Pallas kernels: 44.8 us -> 47.5 us  [the longest x1 43.1 us: local_stack(): pl.pallas_call(kernel, out_shape=(out, out, jax.ShapeDtypeStruct((8, BLOC...]
where the time goes in v2:
time: 48.3 us; the launch traced here: 48.2 us
  Pallas kernels  47.5 us (98%)
  between operations  0.64 us (1%)
    pallas_call x1, Pallas kernels, local_stack(): pl.pallas_call(kernel, out_shape=(out, out, jax.ShapeDtypeStruct((8, BLOC...  43.1 us
    pallas_call x1, Pallas kernels, local_stack(): pl.pallas_call(last_layer, grid=(8 // STEP,), out_shape=(jax.ShapeDtypeSt...  4.43 us

profile of v2, /device:TPU:0, one launch (start us, length us, event | category | flops | bytes accessed | tf_op | source)
XLA Modules:
  0.0 48.2 jit_solution(3142417610821925657)
XLA Ops:
  0.6 43.1 %shard_map.59 = (f32[4,2,128,256]{3,2,1,0:T(8,128)}, f32[4,2,128,256]{3,2,1,0:T(8,128)}, bf16[8,128,256]{2,1,0:T(8,128)(2,1)}) custom-call(bf16[4,2,128,256]{3,2,1,0:T(8,128)(2,1)} %bitcast.7, bf16[10,768,512]{2,1,0:T(8,128)(2,1)} %bitcast.4, bf16[10,256,256]{2,1,0:T(8,128)(2,1)} %wres_ref.1, bf16[10,256,256]{2,1,0:T(8,128)(2,1)} %wskip_ref.1), custom_call_target="tpu_custom_call" | custom-call | tf_op jit(solution)/shard_map/pallas_call | solution.py:237
  43.7 4.4 %shard_map.60 = (f32[8,128,256]{2,1,0:T(8,128)}, f32[8,128,256]{2,1,0:T(8,128)}) custom-call(bf16[8,128,256]{2,1,0:T(8,128)(2,1)} %get-tuple-element.5.a_ref, f32[8,128,256]{2,1,0:T(8,128)} %bitcast.5, f32[8,128,256]{2,1,0:T(8,128)} %bitcast.6, bf16[10,256,256]{2,1,0:T(8,128)(2,1)} %wres_ref.1, bf16[10,256,256]{2,1,0:T(8,128)(2,1)} %wskip_ref.1), custom_call_target="tpu_custom_call" | custom-call | tf_op jit(solution)/shard_map/pallas_call | solution.py:247

commit v3 on v2

--- a/solution.py
+++ b/solution.py
@@ -13,8 +13,8 @@
 LOCAL = 8
 SEQ, BLOCK, CHIP, CHAN = 1024, 128, 256, 256
 TILE = 512
-STEP = 2
-VMEM_LIMIT = 57 * 2 ** 20
+STEP = 4
+VMEM_LIMIT = 50 * 2 ** 20
 
 
 def pad_rows(layer):
@@ -47,7 +47,7 @@
     return jnp.dot(a, b, preferred_element_type=F32)
 
 
-def kernel(x_ref, win_hbm, wres_hbm, wskip_hbm, oh_ref, os_ref, last_ref, *scratch):
+def kernel(x_ref, win_hbm, wres_hbm, wskip_hbm, oh_ref, os_ref, last_ref, wlast_ref, *scratch):
     su = scratch[:LAYERS]
     hu = scratch[LAYERS:LAYERS + LOCAL]
     (win, wres, wskip, hseq, hh, hs, fin_h, fin_s, sa, aland,
@@ -204,7 +204,9 @@
         a = aland[k - LOCAL].reshape(8 * BLOCK, CHAN)
         fin_h[...] = fin_h[...] + dot(a, wres[span, :]).reshape(fin_h.shape)
         fin_s[...] = fin_s[...] + dot(a, wskip[span, :]).reshape(fin_s.shape)
-    outs = [pltpu.make_async_copy(fin_h, oh_ref, osem.at[0]), pltpu.make_async_copy(fin_s, os_ref, osem.at[1])]
+    final = pl.ds((LAYERS - 1) * CHAN, CHAN)
+    outs = [pltpu.make_async_copy(fin_h, oh_ref, osem.at[0]), pltpu.make_async_copy(fin_s, os_ref, osem.at[1]),
+            pltpu.make_async_copy(wres.at[final], wlast_ref.at[0], osem.at[2]), pltpu.make_async_copy(wskip.at[final], wlast_ref.at[1], osem.at[3])]
     for out in outs:
         out.start()
     wait_gated(LAYERS - 1)
@@ -214,10 +216,11 @@
         copy.wait_send()
 
 
-def last_layer(a_ref, h_ref, s_ref, wres_ref, wskip_ref, oh_ref, os_ref):
-    a = a_ref[...].reshape(-1, CHAN)
-    oh_ref[...] = h_ref[...] + dot(a, wres_ref[0]).reshape(h_ref.shape)
-    os_ref[...] = s_ref[...] + dot(a, wskip_ref[0]).reshape(s_ref.shape)
+def last_layer(a_ref, h_ref, s_ref, w_ref, oh_ref, os_ref):
+    here = pl.ds(pl.program_id(0) * STEP, STEP)
+    a = a_ref[here].reshape(STEP * BLOCK, CHAN)
+    oh_ref[...] = h_ref[here] + dot(a, w_ref[0]).reshape(oh_ref.shape)
+    os_ref[...] = s_ref[here] + dot(a, w_ref[1]).reshape(os_ref.shape)
 
 
 def solution(mesh):
@@ -233,23 +236,23 @@
                     vmem((SEQ, CHAN), F32), vmem((2, 4, BLOCK, CHAN), F32), vmem((2, 4, BLOCK, CHAN), F32),
                     vmem((4, 2, BLOCK, CHAN), F32), vmem((4, 2, BLOCK, CHAN), F32),
                     vmem((LAYERS - LOCAL, SEQ, CHAN), BF16), vmem((LAYERS - LOCAL - 1, 8, BLOCK, CHAN), BF16)]
-        scratch += [dma(LAYERS, 3), dma(8), dma(8), dma(2), dma(2), dma(LOCAL, 4, 2), dma(LOCAL, 4, 2), dma(LAYERS - LOCAL, 8), dma(LAYERS - LOCAL, 8), dma(2, 2), dma(2), dma(2)]
-        h, s, a = pl.pallas_call(
+        scratch += [dma(LAYERS, 3), dma(8), dma(8), dma(2), dma(2), dma(LOCAL, 4, 2), dma(LOCAL, 4, 2), dma(LAYERS - LOCAL, 8), dma(LAYERS - LOCAL, 8), dma(2, 2), dma(2), dma(4)]
+        h, s, a, w = pl.pallas_call(
             kernel,
-            out_shape=(out, out, jax.ShapeDtypeStruct((8, BLOCK, CHAN), BF16)),
+            out_shape=(out, out, jax.ShapeDtypeStruct((8, BLOCK, CHAN), BF16), jax.ShapeDtypeStruct((2, CHAN, CHAN), BF16)),
             in_specs=[pl.BlockSpec(memory_space=pltpu.HBM)] * 4,
-            out_specs=(pl.BlockSpec(memory_space=pl.ANY),) * 3,
+            out_specs=(pl.BlockSpec(memory_space=pl.ANY),) * 4,
             scratch_shapes=scratch,
             compiler_params=pltpu.CompilerParams(collective_id=0, has_side_effects=True, vmem_limit_bytes=VMEM_LIMIT),
         )(x.reshape(4, 2, BLOCK, CHAN), w_in.reshape(LAYERS, 3 * CHAN, 2 * CHAN), w_res, w_skip)
         rows = pl.BlockSpec((STEP, BLOCK, CHAN), lambda i: (i, 0, 0))
-        weight = pl.BlockSpec((1, CHAN, CHAN), lambda i: (LAYERS - 1, 0, 0))
         return pl.pallas_call(
             last_layer,
             grid=(8 // STEP,),
             out_shape=(jax.ShapeDtypeStruct(x.shape, F32),) * 2,
-            in_specs=[rows, rows, rows, weight, weight],
+            in_specs=[pl.BlockSpec(memory_space=pltpu.VMEM)] * 4,
             out_specs=(rows, rows),
-        )(a, h.reshape(x.shape), s.reshape(x.shape), w_res, w_skip)
+            compiler_params=pltpu.CompilerParams(vmem_limit_bytes=8 * 2 ** 20),
+        )(a, h.reshape(x.shape), s.reshape(x.shape), w)
 
     return jax.shard_map(local_stack, mesh=mesh, in_specs=(act_spec, P(), P(), P()), out_specs=(act_spec, act_spec), check_vma=False)

time: 48.3 us -> 46.5 us (0.963)
  Pallas kernels: 47.5 us -> 44.7 us
  local copies, waits for them, and re-layouts: 0 us -> 1.03 us
    pallas_call x1, Pallas kernels: 4.43 us -> 1.64 us  [local_stack(): pl.pallas_call(last_layer, grid=(8 // STEP,), out_shape=(jax.ShapeDtypeSt...]
    unnamed x0 -> x2, local copies, waits for them, and re-layouts: none -> 1.03 us
where the time goes in v3:
time: 46.5 us; the launch traced here: 46.4 us
  Pallas kernels  44.7 us (96%)
  local copies, waits for them, and re-layouts  1.03 us (2%)
  between operations  0.65 us (1%)
    pallas_call x1, Pallas kernels, local_stack(): pl.pallas_call(kernel, out_shape=(out, out, jax.ShapeDtypeStruct((8, BLOC...  43.1 us
    pallas_call x1, Pallas kernels, local_stack(): pl.pallas_call(last_layer, grid=(8 // STEP,), out_shape=(jax.ShapeDtypeSt...  1.64 us
    unnamed x2, local copies, waits for them, and re-layouts  1.03 us

profile of v3, /device:TPU:0, one launch (start us, length us, event | category | flops | bytes accessed | tf_op | source)
XLA Modules:
  0.0 46.4 jit_solution(7952332635848477918)
XLA Ops:
  0.6 0.0 copy-start
  0.6 1.0 %copy-done = bf16[8,128,256]{2,1,0:T(8,128)(2,1)S(1)} copy-done((bf16[8,128,256]{2,1,0:T(8,128)(2,1)S(1)}, bf16[8,128,256]{2,1,0:T(8,128)(2,1)}, u32[]{:S(2)}) %copy-start) | copy-done | bytes 524312
  1.7 43.1 %shard_map.59 = (f32[4,2,128,256]{3,2,1,0:T(8,128)S(1)}, f32[4,2,128,256]{3,2,1,0:T(8,128)S(1)}, bf16[8,128,256]{2,1,0:T(8,128)(2,1)S(1)}, bf16[2,256,256]{2,1,0:T(8,128)(2,1)S(1)}) custom-call(bf16[4,2,128,256]{3,2,1,0:T(8,128)(2,1)S(1)} %bitcast.6, bf16[10,768,512]{2,1,0:T(8,128)(2,1)} %bitcast.7, bf16[10,256,256]{2,1,0:T(8,128)(2,1)} %wres_hbm.1, ...), custom_call_target="tpu_custom_call" | custom-call | tf_op jit(solution)/shard_map/pallas_call | solution.py:240
  44.8 1.6 %shard_map.60 = (f32[8,128,256]{2,1,0:T(8,128)}, f32[8,128,256]{2,1,0:T(8,128)}) custom-call(bf16[8,128,256]{2,1,0:T(8,128)(2,1)S(1)} %get-tuple-element.6.a_ref, f32[8,128,256]{2,1,0:T(8,128)S(1)} %bitcast.4, f32[8,128,256]{2,1,0:T(8,128)S(1)} %bitcast.5, bf16[2,256,256]{2,1,0:T(8,128)(2,1)S(1)} %get-tuple-element.9.w_ref), custom_call_target="tpu_custom_call" | custom-call | tf_op jit(solution)/shard_map/pallas_call | solution.py:249
Async XLA Ops:
  0.6 1.0 %copy-start = (bf16[8,128,256]{2,1,0:T(8,128)(2,1)S(1)}, bf16[8,128,256]{2,1,0:T(8,128)(2,1)}, u32[]{:S(2)}) copy-start(bf16[8,128,256]{2,1,0:T(8,128)(2,1)} %param.4) | copy-start | bytes 1572868

commit v4 on v3

v4 whole, which is shorter than its diff:
```python
import functools

import jax
import jax.numpy as jnp
from jax import lax
from jax.experimental import pallas as pl
from jax.experimental.pallas import tpu as pltpu
from jax.sharding import PartitionSpec as P

F32, BF16 = jnp.float32, jnp.bfloat16
MESH = pl.DeviceIdType.MESH
LAYERS = 10
LOCAL = 8
SEQ, BLOCK, CHIP, CHAN = 1024, 128, 256, 256
TILE = 512
STEP = 4
VMEM_LIMIT = 50 * 2 ** 20


EDGE = 128
EXTRA = [128, 128, 128, 112, 96, 64, 0, 0]
MARGIN = [144, 144, 144, 128, 112, 96, 64, 128]


def pad_rows(layer):
    return EDGE if layer == 0 else max(2 ** layer, 16)


def flip(index, q):
    out = index
    for bit in range(3):
        if q >> bit & 1:
            out = out + 2 ** bit - 2 ** (bit + 1) * lax.rem(lax.div(index, 2 ** bit), 2)
    return out


def taps(load, d, n):
    centre = load(0, n)
    if d < 16:
        wide = load(-16, n + 32)
        return jnp.concatenate([wide[16 - d:16 - d + n], centre, wide[16 + d:16 + d + n]], axis=1)
    return jnp.concatenate([load(-d, n), centre, load(d, n)], axis=1)


def gated(z):
    half = jnp.tanh(z[:, CHAN:] * 0.5)
    return (jnp.tanh(z[:, :CHAN]) * (0.5 + 0.5 * half)).astype(BF16)


def dot(a, b):
    return jnp.dot(a, b, preferred_element_type=F32)


def kernel(x_ref, win_hbm, wres_hbm, wskip_hbm, oh_ref, os_ref, last_ref, wlast_ref, *scratch):
    su = scratch[:LAYERS]
    hu = scratch[LAYERS:LAYERS + LOCAL]
    (win, wres, wskip, hseq, hh, hs, own_s, fin_h, fin_s, sa, aland,
     wsem, xsend, xrecv, xloc, psend, precv, hsend, hrecv, asend, arecv, fsend, frecv, floc, osem) = scratch[LAYERS + LOCAL:]

    me = lax.axis_index('sp')
    chip, core = lax.div(me, 2), lax.rem(me, 2)
    partner = flip(me, 1)
    pair = [chip] + [lax.rem(chip + r, 4) for r in (1, 2, 3)]

    def remote(src, dst, send, recv, device):
        return pltpu.make_async_remote_copy(src_ref=src, dst_ref=dst, send_sem=send, recv_sem=recv,
                                            device_id={'sp': device}, device_id_type=MESH)

    def block(start):
        return pl.ds(pl.multiple_of(start, 16), BLOCK)

    weights = []
    for k in range(LAYERS):
        row = [pltpu.make_async_copy(win_hbm.at[k], win.at[k], wsem.at[k, 0]),
               pltpu.make_async_copy(wres_hbm.at[k], wres.at[pl.ds(k * CHAN, CHAN)], wsem.at[k, 1]),
               pltpu.make_async_copy(wskip_hbm.at[k], wskip.at[pl.ds(k * CHAN, CHAN)], wsem.at[k, 2])]
        for copy in row:
            copy.start()
        weights.append(row)

    barrier = pltpu.get_barrier_semaphore()
    for q in range(1, 8):
        pl.semaphore_signal(barrier, inc=1, device_id={'sp': flip(me, q)}, device_id_type=MESH)
    own_rows = block(EDGE + BLOCK * me)
    half_rows = block(MARGIN[0] + BLOCK * core)
    local = [pltpu.make_async_copy(x_ref.at[chip, core], su[0].at[own_rows], xloc.at[0])]
    local += [pltpu.make_async_copy(x_ref.at[pair[r], core], hu[0].at[r - 1, half_rows], xloc.at[r]) for r in (1, 2, 3)]
    for copy in local:
        copy.start()
    for k in range(LAYERS):
        pad = pad_rows(k)
        su[k][:pad, :] = jnp.zeros((pad, CHAN), BF16)
        su[k][pad + SEQ:, :] = jnp.zeros((pad, CHAN), BF16)
    for k in range(3):
        for r in range(3):
            hu[k][r, :16, :] = jnp.zeros((16, CHAN), BF16)
            hu[k][r, CHIP + 2 * MARGIN[k] - 16:, :] = jnp.zeros((16, CHAN), BF16)
    pl.semaphore_wait(barrier, 7)

    spread = []
    for q in (6, 7, 2, 4, 3, 5, 1):
        to = flip(me, q)
        copy = remote(x_ref.at[lax.div(to, 2), lax.rem(to, 2)], su[0].at[own_rows], xsend.at[q], xrecv.at[q], to)
        copy.start()
        spread.append(copy)
    mates = [remote(x_ref.at[pair[r], 1 - core], hu[0].at[r - 1, half_rows], psend.at[r], precv.at[r], partner) for r in (1, 2, 3)]
    for copy in mates:
        copy.start()

    sends = []

    def send_edges(k, n):
        for r in (1, 2, 3):
            for side in range(2):
                src = su[k].at[block(CHIP * pair[r] + side * (CHIP + EDGE))]
                dst = hu[k].at[3 - r, pl.ds(MARGIN[k] - EDGE + side * (CHIP + EDGE), EDGE)]
                copy = remote(src, dst, hsend.at[n, r, side], hrecv.at[n, 3 - r, side], 2 * pair[r] + core)
                copy.start()
                sends.append(copy)

    def wait_edges(k, n):
        for r in range(3):
            for side in range(2):
                dst = hu[k].at[r, pl.ds(MARGIN[k] - EDGE + side * (CHIP + EDGE), EDGE)]
                pltpu.make_async_copy(dst, dst, hrecv.at[n, r, side]).wait()

    def landing(k):
        return last_ref if k == LAYERS - 1 else aland.at[k - LOCAL]

    def send_gated(k):
        for q in range(8):
            to = flip(me, q)
            src = sa.at[k, block(BLOCK * to)]
            dst = landing(k).at[me]
            if q == 0:
                copy = pltpu.make_async_copy(src, dst, arecv.at[k - LOCAL, 0])
            else:
                copy = remote(src, dst, asend.at[k - LOCAL, q], arecv.at[k - LOCAL, q], to)
                sends.append(copy)
            copy.start()

    def wait_gated(k):
        for q in range(8):
            dst = landing(k).at[flip(me, q)]
            pltpu.make_async_copy(dst, dst, arecv.at[k - LOCAL, q]).wait()

    def seq_layer(k):
        d, pad = 2 ** k, pad_rows(k)
        weights[k][0].wait()
        weights[k][1].wait()
        rows = range(0, SEQ, TILE)
        pre = [dot(taps(lambda start, size: su[k][pl.ds(row + pad + start, size), :], d, TILE), win[k]) for row in rows]
        for row, z in zip(rows, pre):
            here = pl.ds(row, TILE)
            a = gated(z)
            sa[k, here, :] = a
            if k < LAYERS - 1:
                new = hseq[here, :] + dot(a, wres[pl.ds(k * CHAN, CHAN), :])
                if k < LOCAL:
                    hseq[here, :] = new
                su[k + 1][pl.ds(row + pad_rows(k + 1), TILE), :] = new.astype(BF16)

    def home_layer(k):
        d, extra, margin = 2 ** k, EXTRA[k], MARGIN[k]
        size = CHIP + 2 * extra
        here = pl.ds(EDGE - extra, size)
        weights[k][2].wait()
        pre = [dot(taps(lambda start, n: hu[k][r, pl.ds(margin - extra + start, n), :], d, size), win[k]) for r in range(3)]
        for r, z in enumerate(pre):
            a = gated(z)
            new = hh[r, here, :] + dot(a, wres[pl.ds(k * CHAN, CHAN), :])
            hh[r, here, :] = new
            skip = dot(a[extra:extra + CHIP], wskip[pl.ds(k * CHAN, CHAN), :])
            hs[r] = skip if k == 0 else hs[r] + skip
            if k < LOCAL - 1:
                base = MARGIN[k + 1]
                hu[k + 1][r, pl.ds(base, CHIP), :] = new[extra:extra + CHIP].astype(BF16)
                if extra:
                    hu[k + 1][r, pl.ds(base - extra, extra), :] = jnp.where(chip > 0, new[:extra], 0.0).astype(BF16)
                    hu[k + 1][r, pl.ds(base + CHIP, extra), :] = jnp.where(chip < 3, new[extra + CHIP:], 0.0).astype(BF16)

    local[0].wait()
    for copy in spread:
        copy.wait()
    send_edges(0, 0)
    hseq[...] = su[0][pl.ds(EDGE, SEQ), :].astype(F32)
    for k in range(LAYERS):
        seq_layer(k)
        if k == LOCAL - 2:
            send_edges(LOCAL - 1, 1)
        if k >= LOCAL:
            send_gated(k)
    for copy in local[1:] + mates:
        copy.wait()
    wait_edges(0, 0)
    for r in range(3):
        hh[r] = hu[0][r, pl.ds(MARGIN[0] - EDGE, CHIP + 2 * EDGE), :].astype(F32)
    for k in range(LOCAL):
        if k == LOCAL - 1:
            wait_edges(k, 1)
        home_layer(k)
    mine = pl.ds(pl.multiple_of(CHIP * chip, CHIP), CHIP)
    own_s[...] = dot(jnp.concatenate([sa[k, mine, :] for k in range(LOCAL)], axis=1), wskip[pl.ds(0, LOCAL * CHAN), :])
    moves = []
    for r in range(4):
        for n, dst in enumerate((fin_h, fin_s)):
            def half(which):
                if r:
                    return (hh.at[r - 1, block(EDGE + BLOCK * which)], hs.at[r - 1, block(BLOCK * which)])[n]
                return (hseq.at[block(CHIP * chip + BLOCK * which)], own_s.at[block(BLOCK * which)])[n]
            moves += [remote(half(1 - core), dst.at[pair[r], core], fsend.at[r, n], frecv.at[r, n], partner),
                      pltpu.make_async_copy(half(core), dst.at[pair[r], core], floc.at[r, n])]
    for move in moves:
        move.start()
    for k in range(LOCAL, LAYERS):
        weights[k][2].wait()
    for move in moves:
        move.wait()
    for k in range(LOCAL, LAYERS - 1):
        wait_gated(k)
        span = pl.ds(k * CHAN, CHAN)
        a = aland[k - LOCAL].reshape(8 * BLOCK, CHAN)
        fin_h[...] = fin_h[...] + dot(a, wres[span, :]).reshape(fin_h.shape)
        fin_s[...] = fin_s[...] + dot(a, wskip[span, :]).reshape(fin_s.shape)
    final = pl.ds((LAYERS - 1) * CHAN, CHAN)
    outs = [pltpu.make_async_copy(fin_h, oh_ref, osem.at[0]), pltpu.make_async_copy(fin_s, os_ref, osem.at[1]),
            pltpu.make_async_copy(wres.at[final], wlast_ref.at[0], osem.at[2]), pltpu.make_async_copy(wskip.at[final], wlast_ref.at[1], osem.at[3])]
    for out in outs:
        out.start()
    wait_gated(LAYERS - 1)
    for out in outs:
        out.wait()
    for copy in sends:
        copy.wait_send()


def last_layer(a_ref, h_ref, s_ref, w_ref, oh_ref, os_ref):
    here = pl.ds(pl.program_id(0) * STEP, STEP)
    a = a_ref[here].reshape(STEP * BLOCK, CHAN)
    oh_ref[...] = h_ref[here] + dot(a, w_ref[0]).reshape(oh_ref.shape)
    os_ref[...] = s_ref[here] + dot(a, w_ref[1]).reshape(os_ref.shape)


def solution(mesh):
    act_spec = P('dp', 'sp', None)

    def local_stack(x, w_in, w_res, w_skip):
        vmem = lambda shape, dtype: pltpu.VMEM(shape, dtype)
        dma = lambda *shape: pltpu.SemaphoreType.DMA(shape)
        out = jax.ShapeDtypeStruct((4, 2, BLOCK, CHAN), F32)
        scratch = [vmem((SEQ + 2 * pad_rows(k), CHAN), BF16) for k in range(LAYERS)]
        scratch += [vmem((3, CHIP + 2 * MARGIN[k], CHAN), BF16) for k in range(LOCAL)]
        scratch += [vmem((LAYERS, 3 * CHAN, 2 * CHAN), BF16), vmem((LAYERS * CHAN, CHAN), BF16), vmem((LAYERS * CHAN, CHAN), BF16),
                    vmem((SEQ, CHAN), F32), vmem((3, CHIP + 2 * EDGE, CHAN), F32), vmem((3, CHIP, CHAN), F32), vmem((CHIP, CHAN), F32),
                    vmem((4, 2, BLOCK, CHAN), F32), vmem((4, 2, BLOCK, CHAN), F32),
                    vmem((LAYERS, SEQ, CHAN), BF16), vmem((LAYERS - LOCAL - 1, 8, BLOCK, CHAN), BF16)]
        scratch += [dma(LAYERS, 3), dma(8), dma(8), dma(4), dma(4), dma(4), dma(2, 4, 2), dma(2, 3, 2),
                    dma(LAYERS - LOCAL, 8), dma(LAYERS - LOCAL, 8), dma(4, 2), dma(4, 2), dma(4, 2), dma(4)]
        h, s, a, w = pl.pallas_call(
            kernel,
            out_shape=(out, out, jax.ShapeDtypeStruct((8, BLOCK, CHAN), BF16), jax.ShapeDtypeStruct((2, CHAN, CHAN), BF16)),
            in_specs=[pl.BlockSpec(memory_space=pltpu.HBM)] * 4,
            out_specs=(pl.BlockSpec(memory_space=pl.ANY),) * 4,
            scratch_shapes=scratch,
            compiler_params=pltpu.CompilerParams(collective_id=0, has_side_effects=True, vmem_limit_bytes=VMEM_LIMIT),
        )(pltpu.with_memory_space_constraint(x.reshape(4, 2, BLOCK, CHAN), pltpu.HBM), w_in.reshape(LAYERS, 3 * CHAN, 2 * CHAN), w_res, w_skip)
        rows = pl.BlockSpec((STEP, BLOCK, CHAN), lambda i: (i, 0, 0))
        return pl.pallas_call(
            last_layer,
            grid=(8 // STEP,),
            out_shape=(jax.ShapeDtypeStruct(x.shape, F32),) * 2,
            in_specs=[pl.BlockSpec(memory_space=pltpu.VMEM)] * 4,
            out_specs=(rows, rows),
            compiler_params=pltpu.CompilerParams(vmem_limit_bytes=8 * 2 ** 20),
        )(a, h.reshape(x.shape), s.reshape(x.shape), w)

    return jax.shard_map(local_stack, mesh=mesh, in_specs=(act_spec, P(), P(), P()), out_specs=(act_spec, act_spec), check_vma=False)
```

time: 46.5 us -> 42.4 us (0.912)
  Pallas kernels: 44.7 us -> 41.7 us
  local copies, waits for them, and re-layouts: 1.03 us -> 0 us
    pallas_call x1, Pallas kernels: 43.1 us -> 40 us  [local_stack(): pl.pallas_call(kernel, out_shape=(out, out, jax.ShapeDtypeStruct((8, BLOC...]
    unnamed x2 -> x0, local copies, waits for them, and re-layouts: 1.03 us -> none
where the time goes in v4:
time: 42.4 us; the launch traced here: 42.3 us
  Pallas kernels  41.7 us (98%)
  between operations  0.64 us (2%)
    pallas_call x1, Pallas kernels, local_stack(): pl.pallas_call(kernel, out_shape=(out, out, jax.ShapeDtypeStruct((8, BLOC...  40 us
    pallas_call x1, Pallas kernels, local_stack(): pl.pallas_call(last_layer, grid=(8 // STEP,), out_shape=(jax.ShapeDtypeSt...  1.63 us

profile of v4, /device:TPU:0, one launch (start us, length us, event | category | flops | bytes accessed | tf_op | source)
XLA Modules:
  0.0 42.3 jit_solution(1445847069128895323)
XLA Ops:
  0.6 40.0 %shard_map.59 = (f32[4,2,128,256]{3,2,1,0:T(8,128)S(1)}, f32[4,2,128,256]{3,2,1,0:T(8,128)S(1)}, bf16[8,128,256]{2,1,0:T(8,128)(2,1)S(1)}, bf16[2,256,256]{2,1,0:T(8,128)(2,1)S(1)}) custom-call(bf16[4,2,128,256]{3,2,1,0:T(8,128)(2,1)} %bitcast.7, bf16[10,768,512]{2,1,0:T(8,128)(2,1)} %bitcast.6, bf16[10,256,256]{2,1,0:T(8,128)(2,1)} %wres_hbm.1, ...), custom_call_target="tpu_custom_call" | custom-call | tf_op jit(solution)/shard_map/pallas_call | solution.py:259
  40.7 1.6 %shard_map.60 = (f32[8,128,256]{2,1,0:T(8,128)}, f32[8,128,256]{2,1,0:T(8,128)}) custom-call(bf16[8,128,256]{2,1,0:T(8,128)(2,1)S(1)} %get-tuple-element.6.a_ref, f32[8,128,256]{2,1,0:T(8,128)S(1)} %bitcast.4, f32[8,128,256]{2,1,0:T(8,128)S(1)} %bitcast.5, bf16[2,256,256]{2,1,0:T(8,128)(2,1)S(1)} %get-tuple-element.9.w_ref), custom_call_target="tpu_custom_call" | custom-call | tf_op jit(solution)/shard_map/pallas_call | solution.py:268

commit v5 on v4

--- a/solution.py
+++ b/solution.py
@@ -13,6 +13,7 @@
 LOCAL = 8
 SEQ, BLOCK, CHIP, CHAN = 1024, 128, 256, 256
 TILE = 512
+EARLY = 3
 STEP = 4
 VMEM_LIMIT = 50 * 2 ** 20
 
@@ -55,7 +56,7 @@
     su = scratch[:LAYERS]
     hu = scratch[LAYERS:LAYERS + LOCAL]
     (win, wres, wskip, hseq, hh, hs, own_s, fin_h, fin_s, sa, aland,
-     wsem, xsend, xrecv, xloc, psend, precv, hsend, hrecv, asend, arecv, fsend, frecv, floc, osem) = scratch[LAYERS + LOCAL:]
+     wsem, xsend, xrecv, xloc, psend, precv, hsend, hrecv, asend, arecv, fsend, frecv, floc, osem, relay) = scratch[LAYERS + LOCAL:]
 
     me = lax.axis_index('sp')
     chip, core = lax.div(me, 2), lax.rem(me, 2)
@@ -79,7 +80,7 @@
         weights.append(row)
 
     barrier = pltpu.get_barrier_semaphore()
-    for q in range(1, 8):
+    for q in range(1, 6):
         pl.semaphore_signal(barrier, inc=1, device_id={'sp': flip(me, q)}, device_id_type=MESH)
     own_rows = block(EDGE + BLOCK * me)
     half_rows = block(MARGIN[0] + BLOCK * core)
@@ -95,14 +96,16 @@
         for r in range(3):
             hu[k][r, :16, :] = jnp.zeros((16, CHAN), BF16)
             hu[k][r, CHIP + 2 * MARGIN[k] - 16:, :] = jnp.zeros((16, CHAN), BF16)
-    pl.semaphore_wait(barrier, 7)
-
-    spread = []
-    for q in (6, 7, 2, 4, 3, 5, 1):
+    pl.semaphore_wait(barrier, 5)
+    pl.semaphore_signal(relay, inc=1, device_id={'sp': flip(me, 2)}, device_id_type=MESH)
+
+    spread = {}
+    for q in (2, 4, 3, 5, 1, 6, 7):
+        if q == 6:
+            pl.semaphore_wait(relay, 1)
         to = flip(me, q)
-        copy = remote(x_ref.at[lax.div(to, 2), lax.rem(to, 2)], su[0].at[own_rows], xsend.at[q], xrecv.at[q], to)
-        copy.start()
-        spread.append(copy)
+        spread[q] = remote(x_ref.at[lax.div(to, 2), lax.rem(to, 2)], su[0].at[own_rows], xsend.at[q], xrecv.at[q], to)
+        spread[q].start()
     mates = [remote(x_ref.at[pair[r], 1 - core], hu[0].at[r - 1, half_rows], psend.at[r], precv.at[r], partner) for r in (1, 2, 3)]
     for copy in mates:
         copy.start()
@@ -144,21 +147,22 @@
             dst = landing(k).at[flip(me, q)]
             pltpu.make_async_copy(dst, dst, arecv.at[k - LOCAL, q]).wait()
 
-    def seq_layer(k):
+    def seq_layer(k, tiles):
         d, pad = 2 ** k, pad_rows(k)
-        weights[k][0].wait()
-        weights[k][1].wait()
-        rows = range(0, SEQ, TILE)
-        pre = [dot(taps(lambda start, size: su[k][pl.ds(row + pad + start, size), :], d, TILE), win[k]) for row in rows]
-        for row, z in zip(rows, pre):
-            here = pl.ds(row, TILE)
+
+        def rows_at(start, size):
+            return pl.ds(start if isinstance(start, int) else pl.multiple_of(start, 16), size)
+
+        pre = [dot(taps(lambda start, n: su[k][rows_at(row + pad + start, n), :], d, size), win[k]) for row, size in tiles]
+        for (row, size), z in zip(tiles, pre):
+            here = rows_at(row, size)
             a = gated(z)
             sa[k, here, :] = a
             if k < LAYERS - 1:
                 new = hseq[here, :] + dot(a, wres[pl.ds(k * CHAN, CHAN), :])
                 if k < LOCAL:
                     hseq[here, :] = new
-                su[k + 1][pl.ds(row + pad_rows(k + 1), TILE), :] = new.astype(BF16)
+                su[k + 1][rows_at(row + pad_rows(k + 1), size), :] = new.astype(BF16)
 
     def home_layer(k):
         d, extra, margin = 2 ** k, EXTRA[k], MARGIN[k]
@@ -179,13 +183,30 @@
                     hu[k + 1][r, pl.ds(base - extra, extra), :] = jnp.where(chip > 0, new[:extra], 0.0).astype(BF16)
                     hu[k + 1][r, pl.ds(base + CHIP, extra), :] = jnp.where(chip < 3, new[extra + CHIP:], 0.0).astype(BF16)
 
+    low = lax.div(chip, 2)
     local[0].wait()
-    for copy in spread:
-        copy.wait()
+    for q in (1, 2, 3):
+        spread[q].wait()
+    near, far = (pl.multiple_of(which * TILE, 16) for which in (low, 1 - low))
+    hseq[pl.ds(near, TILE), :] = su[0][pl.ds(pl.multiple_of(EDGE + near, 16), TILE), :].astype(F32)
+    for k in range(EARLY):
+        weights[k][0].wait()
+        weights[k][1].wait()
+        size = TILE - 16 * (k + 1)
+        seq_layer(k, [(low * (SEQ - size), size)])
+    for q in (4, 5, 6, 7):
+        spread[q].wait()
     send_edges(0, 0)
-    hseq[...] = su[0][pl.ds(EDGE, SEQ), :].astype(F32)
+    hseq[pl.ds(far, TILE), :] = su[0][pl.ds(pl.multiple_of(EDGE + far, 16), TILE), :].astype(F32)
     for k in range(LAYERS):
-        seq_layer(k)
+        if k < EARLY:
+            size = TILE + 16 * (k + 1)
+            start, part = (1 - low) * (SEQ - size), 16 * (size // 32)
+            seq_layer(k, [(start, part), (start + part, size - part)])
+        else:
+            weights[k][0].wait()
+            weights[k][1].wait()
+            seq_layer(k, [(row, TILE) for row in range(0, SEQ, TILE)])
         if k == LOCAL - 2:
             send_edges(LOCAL - 1, 1)
         if k >= LOCAL:
@@ -255,7 +276,7 @@
                     vmem((4, 2, BLOCK, CHAN), F32), vmem((4, 2, BLOCK, CHAN), F32),
                     vmem((LAYERS, SEQ, CHAN), BF16), vmem((LAYERS - LOCAL - 1, 8, BLOCK, CHAN), BF16)]
         scratch += [dma(LAYERS, 3), dma(8), dma(8), dma(4), dma(4), dma(4), dma(2, 4, 2), dma(2, 3, 2),
-                    dma(LAYERS - LOCAL, 8), dma(LAYERS - LOCAL, 8), dma(4, 2), dma(4, 2), dma(4, 2), dma(4)]
+                    dma(LAYERS - LOCAL, 8), dma(LAYERS - LOCAL, 8), dma(4, 2), dma(4, 2), dma(4, 2), dma(4), pltpu.SemaphoreType.REGULAR]
         h, s, a, w = pl.pallas_call(
             kernel,
             out_shape=(out, out, jax.ShapeDtypeStruct((8, BLOCK, CHAN), BF16), jax.ShapeDtypeStruct((2, CHAN, CHAN), BF16)),

time: 42.4 us -> 41.4 us (0.976)
  Pallas kernels: 41.7 us -> 40.7 us
    pallas_call x1, Pallas kernels: 40 us -> 39 us  [local_stack(): pl.pallas_call(kernel, out_shape=(out, out, jax.ShapeDtypeStruct((8, BLOC...]
where the time goes in v5:
time: 41.4 us; the launch traced here: 41.3 us
  Pallas kernels  40.7 us (98%)
  between operations  0.64 us (2%)
    pallas_call x1, Pallas kernels, local_stack(): pl.pallas_call(kernel, out_shape=(out, out, jax.ShapeDtypeStruct((8, BLOC...  39 us
    pallas_call x1, Pallas kernels, local_stack(): pl.pallas_call(last_layer, grid=(8 // STEP,), out_shape=(jax.ShapeDtypeSt...  1.63 us

profile of v5, /device:TPU:0, one launch (start us, length us, event | category | flops | bytes accessed | tf_op | source)
XLA Modules:
  0.0 41.3 jit_solution(7437839596239637961)
XLA Ops:
  0.6 39.0 %shard_map.59 = (f32[4,2,128,256]{3,2,1,0:T(8,128)S(1)}, f32[4,2,128,256]{3,2,1,0:T(8,128)S(1)}, bf16[8,128,256]{2,1,0:T(8,128)(2,1)S(1)}, bf16[2,256,256]{2,1,0:T(8,128)(2,1)S(1)}) custom-call(bf16[4,2,128,256]{3,2,1,0:T(8,128)(2,1)} %bitcast.7, bf16[10,768,512]{2,1,0:T(8,128)(2,1)} %bitcast.6, bf16[10,256,256]{2,1,0:T(8,128)(2,1)} %wres_hbm.1, ...), custom_call_target="tpu_custom_call" | custom-call | tf_op jit(solution)/shard_map/pallas_call | solution.py:280
  39.7 1.6 %shard_map.60 = (f32[8,128,256]{2,1,0:T(8,128)}, f32[8,128,256]{2,1,0:T(8,128)}) custom-call(bf16[8,128,256]{2,1,0:T(8,128)(2,1)S(1)} %get-tuple-element.6.a_ref, f32[8,128,256]{2,1,0:T(8,128)S(1)} %bitcast.4, f32[8,128,256]{2,1,0:T(8,128)S(1)} %bitcast.5, bf16[2,256,256]{2,1,0:T(8,128)(2,1)S(1)} %get-tuple-element.9.w_ref), custom_call_target="tpu_custom_call" | custom-call | tf_op jit(solution)/shard_map/pallas_call | solution.py:289

commit v6 on v5

v6 whole, which is shorter than its diff:
```python
import functools

import jax
import jax.numpy as jnp
from jax import lax
from jax.experimental import pallas as pl
from jax.experimental.pallas import tpu as pltpu
from jax.sharding import PartitionSpec as P

F32, BF16 = jnp.float32, jnp.bfloat16
MESH = pl.DeviceIdType.MESH
LAYERS = 10
LOCAL = 8
SEQ, BLOCK, CHIP, CHAN = 1024, 128, 256, 256
TILE = 512
INNER = 3
EARLY = 3
STEP = 4
VMEM_LIMIT = 50 * 2 ** 20


HALO = 160
EXTRA = [max(HALO - 2 ** (k + 1) + 15, 0) // 16 * 16 for k in range(LOCAL)]
MARGIN = [EXTRA[k] + max(2 ** k, 16) for k in range(LOCAL)]
EDGE = MARGIN[-1] - EXTRA[-2]


def pad_rows(layer):
    return max(2 ** layer, 16)


def flip(index, q):
    out = index
    for bit in range(3):
        if q >> bit & 1:
            out = out + 2 ** bit - 2 ** (bit + 1) * lax.rem(lax.div(index, 2 ** bit), 2)
    return out


def taps(load, d, n):
    centre = load(0, n)
    if d < 16:
        wide = load(-16, n + 32)
        return jnp.concatenate([wide[16 - d:16 - d + n], centre, wide[16 + d:16 + d + n]], axis=1)
    return jnp.concatenate([load(-d, n), centre, load(d, n)], axis=1)


def gated(z):
    half = jnp.tanh(z[:, CHAN:] * 0.5)
    return (jnp.tanh(z[:, :CHAN]) * (0.5 + 0.5 * half)).astype(BF16)


def dot(a, b):
    return jnp.dot(a, b, preferred_element_type=F32)


def kernel(x_ref, win_hbm, wres_hbm, wskip_hbm, oh_ref, os_ref, a_ref, w_ref, *scratch):
    su = scratch[:LAYERS]
    hu = scratch[LAYERS:LAYERS + LOCAL]
    (win, wres, wskip, hseq, hh, hs, own_s, sa,
     wsem, xsend, xrecv, xloc, psend, precv, hsend, hrecv, asend, arecv, fsend, frecv, floc, osem, relay) = scratch[LAYERS + LOCAL:]

    me = lax.axis_index('sp')
    chip, core = lax.div(me, 2), lax.rem(me, 2)
    partner = flip(me, 1)
    pair = [chip] + [lax.rem(chip + r, 4) for r in (1, 2, 3)]

    def remote(src, dst, send, recv, device):
        return pltpu.make_async_remote_copy(src_ref=src, dst_ref=dst, send_sem=send, recv_sem=recv,
                                            device_id={'sp': device}, device_id_type=MESH)

    def block(start, size=BLOCK):
        return pl.ds(pl.multiple_of(start, 16), size)

    weights = []
    for k in range(LAYERS):
        row = [pltpu.make_async_copy(win_hbm.at[k], win.at[k], wsem.at[k, 0]),
               pltpu.make_async_copy(wres_hbm.at[k], wres.at[pl.ds(k * CHAN, CHAN)], wsem.at[k, 1]),
               pltpu.make_async_copy(wskip_hbm.at[k], wskip.at[pl.ds(k * CHAN, CHAN)], wsem.at[k, 2])]
        for copy in row:
            copy.start()
        weights.append(row)

    barrier = pltpu.get_barrier_semaphore()
    for q in range(1, 6):
        pl.semaphore_signal(barrier, inc=1, device_id={'sp': flip(me, q)}, device_id_type=MESH)
    own_rows = block(16 + BLOCK * me)
    half_rows = block(MARGIN[0] + BLOCK * core)
    local = [pltpu.make_async_copy(x_ref.at[chip, core], su[0].at[own_rows], xloc.at[0])]
    local += [pltpu.make_async_copy(x_ref.at[pair[r], core], hu[0].at[r - 1, half_rows], xloc.at[r]) for r in (1, 2, 3)]
    for copy in local:
        copy.start()
    for k in range(LAYERS):
        pad = pad_rows(k)
        su[k][:pad, :] = jnp.zeros((pad, CHAN), BF16)
        su[k][pad + SEQ:, :] = jnp.zeros((pad, CHAN), BF16)
    for k in range(3):
        assert MARGIN[k] == 16 + (EXTRA[k - 1] if k else HALO)
        for r in range(3):
            hu[k][r, :16, :] = jnp.zeros((16, CHAN), BF16)
            hu[k][r, CHIP + 2 * MARGIN[k] - 16:, :] = jnp.zeros((16, CHAN), BF16)
    pl.semaphore_wait(barrier, 5)
    pl.semaphore_signal(relay, inc=1, device_id={'sp': flip(me, 2)}, device_id_type=MESH)

    spread = {}
    for q in (2, 4, 3, 5, 1, 6, 7):
        if q == 6:
            pl.semaphore_wait(relay, 1)
        to = flip(me, q)
        spread[q] = remote(x_ref.at[lax.div(to, 2), lax.rem(to, 2)], su[0].at[own_rows], xsend.at[q], xrecv.at[q], to)
        spread[q].start()
    mates = [remote(x_ref.at[pair[r], 1 - core], hu[0].at[r - 1, half_rows], psend.at[r], precv.at[r], partner) for r in (1, 2, 3)]
    for copy in mates:
        copy.start()

    sends = []

    def start_if(cond, copy):
        pl.when(cond)(copy.start)
        sends.append((cond, copy))

    parts = [(0, BLOCK), (1, HALO - BLOCK)] if HALO > BLOCK else [(0, BLOCK)]

    def halo(slot, side, part):
        left = MARGIN[0] - (HALO if part else BLOCK)
        right = MARGIN[0] + CHIP + (BLOCK if part else 0)
        return hu[0].at[slot, block(left + side * (right - left), parts[part][1])]

    for part, size in parts:
        side = core if part else 1 - core
        to_chip = chip + 1 - 2 * side
        slot = 2 - 2 * lax.rem(to_chip + 2, 2)
        rows = block((1 - side) * (BLOCK - size), size)
        for p in range(2):
            copy = remote(x_ref.at[jnp.clip(3 - to_chip, 0, 3), p, rows], halo(slot, side, part), hsend.at[0, p, part],
                          hrecv.at[part, slot, side], jnp.clip(2 * to_chip + p, 0, 7))
            start_if(jnp.logical_and(to_chip >= 0, to_chip <= 3), copy)

    def send_halo():
        for n, q in enumerate((2, 4)):
            to = flip(me, q)
            there = lax.div(to, 2)
            slot = 2 * lax.rem(there, 2) if q == 2 else 1
            for side in range(2):
                for part, size in parts:
                    first = CHIP + part * BLOCK if side else -(HALO if part else BLOCK)
                    src = block(jnp.clip(16 + CHIP * there + first, 0, 32 + SEQ - size), size)
                    copy = remote(su[0].at[src], halo(slot, side, part), hsend.at[1 + part, n, side], hrecv.at[part, slot, side], to)
                    start_if(there < 3 if side else there > 0, copy)

    def wait_halo(side):
        for r in range(3):
            for part, _ in parts:
                dst = halo(r, side, part)
                pltpu.make_async_copy(dst, dst, hrecv.at[part, r, side]).wait()

    last = LOCAL - 1

    def edge(slot, side):
        return hu[last].at[slot, pl.ds(side * (CHIP + 2 * MARGIN[last] - EDGE), EDGE)]

    def send_edges():
        for r in (1, 2, 3):
            for side in range(2):
                src = su[last].at[block(CHIP * pair[r] + side * (CHIP + 2 * MARGIN[last] - EDGE), EDGE)]
                copy = remote(src, edge(3 - r, side), hsend.at[3, r, side], hrecv.at[2, 3 - r, side], 2 * pair[r] + core)
                copy.start()
                sends.append((None, copy))

    def wait_edges():
        for r in range(3):
            for side in range(2):
                dst = edge(r, side)
                pltpu.make_async_copy(dst, dst, hrecv.at[2, r, side]).wait()

    def send_gated(k):
        for q in range(8):
            to = flip(me, q)
            src = sa.at[k, block(BLOCK * to)]
            dst = a_ref.at[k - LOCAL, me]
            if q == 0:
                copy = pltpu.make_async_copy(src, dst, arecv.at[k - LOCAL, 0])
            else:
                copy = remote(src, dst, asend.at[k - LOCAL, q], arecv.at[k - LOCAL, q], to)
                sends.append((None, copy))
            copy.start()

    def wait_gated(k):
        for q in range(8):
            dst = a_ref.at[k - LOCAL, flip(me, q)]
            pltpu.make_async_copy(dst, dst, arecv.at[k - LOCAL, q]).wait()

    def seq_layer(k, tiles):
        d, pad = 2 ** k, pad_rows(k)

        def rows_at(start, size):
            return pl.ds(start if isinstance(start, int) else pl.multiple_of(start, 16), size)

        pre = []
        for row, size in tiles:
            rows, weight = taps(lambda start, n: su[k][rows_at(row + pad + start, n), :], d, size), win[k]
            if d == TILE:
                first = 0 if row else CHAN
                rows, weight = rows[:, first:first + 2 * CHAN], win[k, pl.ds(first, 2 * CHAN), :]
            pre.append(dot(rows, weight))
        for (row, size), z in zip(tiles, pre):
            here = rows_at(row, size)
            a = gated(z)
            sa[k, here, :] = a
            if k < LAYERS - 1:
                new = hseq[here, :] + dot(a, wres[pl.ds(k * CHAN, CHAN), :])
                if k < LOCAL:
                    hseq[here, :] = new
                su[k + 1][rows_at(row + pad_rows(k + 1), size), :] = new.astype(BF16)

    moves = []

    def hand_over(r):
        for n, dst in enumerate((oh_ref, os_ref)):
            def half(which):
                if r:
                    return (hh.at[r - 1, block(HALO + BLOCK * which)], hs.at[r - 1, block(BLOCK * which)])[n]
                return (hseq.at[block(CHIP * chip + BLOCK * which)], own_s.at[block(BLOCK * which)])[n]
            pair_of = [remote(half(1 - core), dst.at[pair[r], core], fsend.at[r, n], frecv.at[r, n], partner),
                       pltpu.make_async_copy(half(core), dst.at[pair[r], core], floc.at[r, n])]
            for move in pair_of:
                move.start()
            moves.extend(pair_of)

    def home_layer(k, ranges):
        d, margin = 2 ** k, MARGIN[k]
        weight = pl.ds(k * CHAN, CHAN)
        pre = [dot(jnp.concatenate([taps(lambda start, n: hu[k][r, pl.ds(margin + first + start, n), :], d, size) for first, size in ranges], axis=0), win[k])
               for r in range(3)]
        for r, z in enumerate(pre):
            a = gated(z)
            res = dot(a, wres[weight, :])
            at = 0
            for first, size in ranges:
                here = pl.ds(HALO + first, size)
                new = hh[r, here, :] + res[at:at + size]
                hh[r, here, :] = new
                for low_row, high_row, inside in ((first, 0, chip > 0), (max(first, 0), min(first + size, CHIP), None), (CHIP, first + size, chip < 3)):
                    if low_row < high_row and k < LOCAL - 1:
                        part = new[low_row - first:high_row - first]
                        part = part if inside is None else jnp.where(inside, part, 0.0)
                        hu[k + 1][r, pl.ds(MARGIN[k + 1] + low_row, high_row - low_row), :] = part.astype(BF16)
                at += size
            at = 0
            for first, size in ranges:
                low_row, high_row = max(first, 0), min(first + size, CHIP)
                skip = dot(a[at + low_row - first:at + high_row - first], wskip[weight, :])
                rows = pl.ds(low_row, high_row - low_row)
                hs[r, rows, :] = skip if k == 0 else hs[r, rows, :] + skip
                at += size
            if k == LOCAL - 1:
                hand_over(r + 1)

    for copy in local[1:] + mates:
        copy.wait()
    for r in range(3):
        hh[r, pl.ds(HALO, CHIP), :] = hu[0][r, pl.ds(MARGIN[0], CHIP), :].astype(F32)
    for k in range(INNER):
        for copy in weights[k]:
            copy.wait()
        home_layer(k, [(16 * (k + 1), CHIP - 32 * (k + 1))])
    low = lax.div(chip, 2)
    local[0].wait()
    for q in (1, 2, 3):
        spread[q].wait()
    near, far = (pl.multiple_of(which * TILE, 16) for which in (low, 1 - low))
    hseq[pl.ds(near, TILE), :] = su[0][pl.ds(pl.multiple_of(16 + near, 16), TILE), :].astype(F32)
    for k in range(EARLY):
        if k >= INNER:
            weights[k][0].wait()
            weights[k][1].wait()
        size = TILE - 16 * (k + 1)
        seq_layer(k, [(low * (SEQ - size), size)])
    for q in (4, 5, 6, 7):
        spread[q].wait()
    send_halo()
    hseq[pl.ds(far, TILE), :] = su[0][pl.ds(pl.multiple_of(16 + far, 16), TILE), :].astype(F32)
    for k in range(LAYERS):
        if k < EARLY:
            size = TILE + 16 * (k + 1)
            start, part = (1 - low) * (SEQ - size), 16 * (size // 32)
            seq_layer(k, [(start, part), (start + part, size - part)])
        else:
            if k >= INNER:
                weights[k][0].wait()
                weights[k][1].wait()
            seq_layer(k, [(row, TILE) for row in range(0, SEQ, TILE)])
        if k == LOCAL - 2:
            send_edges()
        if k >= LOCAL:
            send_gated(k)
    for k in range(INNER, LAYERS):
        weights[k][2].wait()
    final = pl.ds(LOCAL * CHAN, (LAYERS - LOCAL) * CHAN)
    outs = [pltpu.make_async_copy(w.at[final], w_ref.at[n], osem.at[n]) for n, w in enumerate((wres, wskip))]
    for out in outs:
        out.start()
    mine = pl.ds(pl.multiple_of(CHIP * chip, CHIP), CHIP)
    own_s[...] = dot(jnp.concatenate([sa[k, mine, :] for k in range(LOCAL)], axis=1), wskip[pl.ds(0, LOCAL * CHAN), :])
    hand_over(0)
    for side, outer in enumerate((chip == 0, chip == 3)):
        @pl.when(outer)
        def _():
            for r in range(3):
                hu[0][r, pl.ds(16 + side * (CHIP + HALO), HALO), :] = jnp.zeros((HALO, CHAN), BF16)

        @pl.when(jnp.logical_not(outer))
        def _():
            wait_halo(side)
    for r in range(3):
        for first in (-HALO, CHIP):
            hh[r, pl.ds(HALO + first, HALO), :] = hu[0][r, pl.ds(MARGIN[0] + first, HALO), :].astype(F32)
    for k in range(LOCAL):
        if k == LOCAL - 1:
            wait_edges()
        if k < INNER:
            done = 16 * (k + 1)
            home_layer(k, [(-EXTRA[k], EXTRA[k] + done), (CHIP - done, done + EXTRA[k])])
        else:
            home_layer(k, [(-EXTRA[k], CHIP + 2 * EXTRA[k])])
    for out in outs:
        out.wait()
    for move in moves:
        move.wait()
    for k in range(LOCAL, LAYERS):
        wait_gated(k)
    for cond, copy in sends:
        if cond is None:
            copy.wait_send()
        else:
            pl.when(cond)(copy.wait_send)


def last_layers(a_ref, h_ref, s_ref, w_ref, oh_ref, os_ref):
    here = pl.ds(pl.program_id(0) * STEP, STEP)
    a = jnp.concatenate([a_ref[n, here].reshape(STEP * BLOCK, CHAN) for n in range(LAYERS - LOCAL)], axis=1)
    oh_ref[...] = h_ref[here] + dot(a, w_ref[0]).reshape(oh_ref.shape)
    os_ref[...] = s_ref[here] + dot(a, w_ref[1]).reshape(os_ref.shape)


def solution(mesh):
    act_spec = P('dp', 'sp', None)

    def local_stack(x, w_in, w_res, w_skip):
        vmem = lambda shape, dtype: pltpu.VMEM(shape, dtype)
        dma = lambda *shape: pltpu.SemaphoreType.DMA(shape)
        out = jax.ShapeDtypeStruct((4, 2, BLOCK, CHAN), F32)
        scratch = [vmem((SEQ + 2 * pad_rows(k), CHAN), BF16) for k in range(LAYERS)]
        scratch += [vmem((3, CHIP + 2 * MARGIN[k], CHAN), BF16) for k in range(LOCAL)]
        scratch += [vmem((LAYERS, 3 * CHAN, 2 * CHAN), BF16), vmem((LAYERS * CHAN, CHAN), BF16), vmem((LAYERS * CHAN, CHAN), BF16),
                    vmem((SEQ, CHAN), F32), vmem((3, CHIP + 2 * HALO, CHAN), F32), vmem((3, CHIP, CHAN), F32), vmem((CHIP, CHAN), F32),
                    vmem((LAYERS, SEQ, CHAN), BF16)]
        scratch += [dma(LAYERS, 3), dma(8), dma(8), dma(4), dma(4), dma(4), dma(4, 4, 2), dma(3, 3, 2),
                    dma(LAYERS - LOCAL, 8), dma(LAYERS - LOCAL, 8), dma(4, 2), dma(4, 2), dma(4, 2), dma(2), pltpu.SemaphoreType.REGULAR]
        h, s, a, w = pl.pallas_call(
            kernel,
            out_shape=(out, out, jax.ShapeDtypeStruct((LAYERS - LOCAL, 8, BLOCK, CHAN), BF16),
                       jax.ShapeDtypeStruct((2, (LAYERS - LOCAL) * CHAN, CHAN), BF16)),
            in_specs=[pl.BlockSpec(memory_space=pltpu.HBM)] * 4,
            out_specs=(pl.BlockSpec(memory_space=pl.ANY),) * 4,
            scratch_shapes=scratch,
            compiler_params=pltpu.CompilerParams(collective_id=0, has_side_effects=True, vmem_limit_bytes=VMEM_LIMIT),
        )(pltpu.with_memory_space_constraint(x.reshape(4, 2, BLOCK, CHAN), pltpu.HBM), w_in.reshape(LAYERS, 3 * CHAN, 2 * CHAN), w_res, w_skip)
        rows = pl.BlockSpec((STEP, BLOCK, CHAN), lambda i: (i, 0, 0))
        return pl.pallas_call(
            last_layers,
            grid=(8 // STEP,),
            out_shape=(jax.ShapeDtypeStruct(x.shape, F32),) * 2,
            in_specs=[pl.BlockSpec(memory_space=pltpu.VMEM)] * 4,
            out_specs=(rows, rows),
            compiler_params=pltpu.CompilerParams(vmem_limit_bytes=8 * 2 ** 20),
        )(a, h.reshape(x.shape), s.reshape(x.shape), w)

    return jax.shard_map(local_stack, mesh=mesh, in_specs=(act_spec, P(), P(), P()), out_specs=(act_spec, act_spec), check_vma=False)
```

time: 41.4 us -> 40.4 us (0.976)
  Pallas kernels: 40.7 us -> 39.6 us
    pallas_call x2, Pallas kernels: 40.7 us -> 39.6 us  [the longest x1 37.8 us: local_stack(): pl.pallas_call(kernel, out_shape=(out, out, jax.ShapeDtypeStruct((LAYERS...]
where the time goes in v6:
time: 40.4 us; the launch traced here: 40.3 us
  Pallas kernels  39.6 us (98%)
  between operations  0.64 us (2%)
    pallas_call x1, Pallas kernels, local_stack(): pl.pallas_call(kernel, out_shape=(out, out, jax.ShapeDtypeStruct((LAYERS...  37.8 us
    pallas_call x1, Pallas kernels, local_stack(): pl.pallas_call(last_layers, grid=(8 // STEP,), out_shape=(jax.ShapeDtypeS...  1.88 us

profile of v6, /device:TPU:0, one launch (start us, length us, event | category | flops | bytes accessed | tf_op | source)
XLA Modules:
  0.0 40.3 jit_solution(8583444233964272673)
XLA Ops:
  0.6 37.8 %shard_map.59 = (f32[4,2,128,256]{3,2,1,0:T(8,128)S(1)}, f32[4,2,128,256]{3,2,1,0:T(8,128)S(1)}, bf16[2,8,128,256]{3,2,1,0:T(8,128)(2,1)S(1)}, bf16[2,512,256]{2,1,0:T(8,128)(2,1)S(1)}) custom-call(bf16[4,2,128,256]{3,2,1,0:T(8,128)(2,1)} %bitcast.7, bf16[10,768,512]{2,1,0:T(8,128)(2,1)} %bitcast.6, bf16[10,256,256]{2,1,0:T(8,128)(2,1)} %wres_hbm.1, ...), custom_call_target="tpu_custom_call" | custom-call | tf_op jit(solution)/shard_map/pallas_call | solution.py:360
  38.4 1.9 %shard_map.60 = (f32[8,128,256]{2,1,0:T(8,128)}, f32[8,128,256]{2,1,0:T(8,128)}) custom-call(bf16[2,8,128,256]{3,2,1,0:T(8,128)(2,1)S(1)} %get-tuple-element.6.a_ref, f32[8,128,256]{2,1,0:T(8,128)S(1)} %bitcast.4, f32[8,128,256]{2,1,0:T(8,128)S(1)} %bitcast.5, bf16[2,512,256]{2,1,0:T(8,128)(2,1)S(1)} %get-tuple-element.9.w_ref), custom_call_target="tpu_custom_call" | custom-call | tf_op jit(solution)/shard_map/pallas_call | solution.py:370

commit v7 on v6

--- a/solution.py
+++ b/solution.py
@@ -14,8 +14,8 @@
 SEQ, BLOCK, CHIP, CHAN = 1024, 128, 256, 256
 TILE = 512
 INNER = 3
-EARLY = 3
-STEP = 4
+EARLY = 4
+STEP = 1
 VMEM_LIMIT = 50 * 2 ** 20
 
 
@@ -102,6 +102,10 @@
     pl.semaphore_wait(barrier, 5)
     pl.semaphore_signal(relay, inc=1, device_id={'sp': flip(me, 2)}, device_id_type=MESH)
 
+    mates = [remote(x_ref.at[pair[r], 1 - core], hu[0].at[r - 1, half_rows], psend.at[r], precv.at[r], partner) for r in (1, 2, 3)]
+    for copy in mates:
+        copy.start()
+
     spread = {}
     for q in (2, 4, 3, 5, 1, 6, 7):
         if q == 6:
@@ -109,10 +113,6 @@
         to = flip(me, q)
         spread[q] = remote(x_ref.at[lax.div(to, 2), lax.rem(to, 2)], su[0].at[own_rows], xsend.at[q], xrecv.at[q], to)
         spread[q].start()
-    mates = [remote(x_ref.at[pair[r], 1 - core], hu[0].at[r - 1, half_rows], psend.at[r], precv.at[r], partner) for r in (1, 2, 3)]
-    for copy in mates:
-        copy.start()
-
     sends = []
 
     def start_if(cond, copy):
@@ -336,11 +336,17 @@
             pl.when(cond)(copy.wait_send)
 
 
-def last_layers(a_ref, h_ref, s_ref, w_ref, oh_ref, os_ref):
-    here = pl.ds(pl.program_id(0) * STEP, STEP)
-    a = jnp.concatenate([a_ref[n, here].reshape(STEP * BLOCK, CHAN) for n in range(LAYERS - LOCAL)], axis=1)
-    oh_ref[...] = h_ref[here] + dot(a, w_ref[0]).reshape(oh_ref.shape)
-    os_ref[...] = s_ref[here] + dot(a, w_ref[1]).reshape(os_ref.shape)
+def last_layers(a_ref, h_ref, s_ref, w_ref, oh_ref, os_ref, h_new, s_new, sem):
+    copies = []
+    for i in range(0, 8, STEP):
+        here = pl.ds(i, STEP)
+        a = jnp.concatenate([a_ref[n, here].reshape(STEP * BLOCK, CHAN) for n in range(LAYERS - LOCAL)], axis=1)
+        for n, (old, new, out) in enumerate(((h_ref, h_new, oh_ref), (s_ref, s_new, os_ref))):
+            new[here] = old[here] + dot(a, w_ref[n]).reshape(STEP, BLOCK, CHAN)
+            copies.append(pltpu.make_async_copy(new.at[here], out.at[here], sem.at[n, i]))
+            copies[-1].start()
+    for copy in copies:
+        copy.wait()
 
 
 def solution(mesh):
@@ -366,13 +372,12 @@
             scratch_shapes=scratch,
             compiler_params=pltpu.CompilerParams(collective_id=0, has_side_effects=True, vmem_limit_bytes=VMEM_LIMIT),
         )(pltpu.with_memory_space_constraint(x.reshape(4, 2, BLOCK, CHAN), pltpu.HBM), w_in.reshape(LAYERS, 3 * CHAN, 2 * CHAN), w_res, w_skip)
-        rows = pl.BlockSpec((STEP, BLOCK, CHAN), lambda i: (i, 0, 0))
         return pl.pallas_call(
             last_layers,
-            grid=(8 // STEP,),
             out_shape=(jax.ShapeDtypeStruct(x.shape, F32),) * 2,
             in_specs=[pl.BlockSpec(memory_space=pltpu.VMEM)] * 4,
-            out_specs=(rows, rows),
+            out_specs=(pl.BlockSpec(memory_space=pl.ANY),) * 2,
+            scratch_shapes=[vmem(x.shape, F32), vmem(x.shape, F32), dma(2, 8)],
             compiler_params=pltpu.CompilerParams(vmem_limit_bytes=8 * 2 ** 20),
         )(a, h.reshape(x.shape), s.reshape(x.shape), w)
 

time: 40.4 us -> 39.9 us (0.988)
  Pallas kernels: 39.6 us -> 39 us
    pallas_call x1, Pallas kernels: 37.8 us -> 37.3 us  [local_stack(): pl.pallas_call(kernel, out_shape=(out, out, jax.ShapeDtypeStruct((LAYERS...]
where the time goes in v7:
time: 39.9 us; the launch traced here: 39.8 us
  Pallas kernels  39 us (98%)
  between operations  0.8 us (2%)
    pallas_call x1, Pallas kernels, local_stack(): pl.pallas_call(kernel, out_shape=(out, out, jax.ShapeDtypeStruct((LAYERS...  37.3 us
    pallas_call x1, Pallas kernels, local_stack(): pl.pallas_call(last_layers, out_shape=(jax.ShapeDtypeStruct(x.shape, F32)...  1.68 us

profile of v7, /device:TPU:0, one launch (start us, length us, event | category | flops | bytes accessed | tf_op | source)
XLA Modules:
  0.0 39.8 jit_solution(15551344378372785200)
XLA Ops:
  0.6 37.3 %shard_map.59 = (f32[4,2,128,256]{3,2,1,0:T(8,128)S(1)}, f32[4,2,128,256]{3,2,1,0:T(8,128)S(1)}, bf16[2,8,128,256]{3,2,1,0:T(8,128)(2,1)S(1)}, bf16[2,512,256]{2,1,0:T(8,128)(2,1)S(1)}) custom-call(bf16[4,2,128,256]{3,2,1,0:T(8,128)(2,1)} %bitcast.7, bf16[10,768,512]{2,1,0:T(8,128)(2,1)} %bitcast.6, bf16[10,256,256]{2,1,0:T(8,128)(2,1)} %wres_hbm.1, ...), custom_call_target="tpu_custom_call" | custom-call | tf_op jit(solution)/shard_map/pallas_call | solution.py:366
  38.0 1.7 %shard_map.60 = (f32[8,128,256]{2,1,0:T(8,128)}, f32[8,128,256]{2,1,0:T(8,128)}) custom-call(bf16[2,8,128,256]{3,2,1,0:T(8,128)(2,1)S(1)} %get-tuple-element.6.a_ref, f32[8,128,256]{2,1,0:T(8,128)S(1)} %bitcast.4, f32[8,128,256]{2,1,0:T(8,128)S(1)} %bitcast.5, bf16[2,512,256]{2,1,0:T(8,128)(2,1)S(1)} %get-tuple-element.9.w_ref), custom_call_target="tpu_custom_call" | custom-call | tf_op jit(solution)/shard_map/pallas_call | solution.py:375

commit v8 on v7

--- a/solution.py
+++ b/solution.py
@@ -107,7 +107,7 @@
         copy.start()
 
     spread = {}
-    for q in (2, 4, 3, 5, 1, 6, 7):
+    for q in (2, 3, 1, 4, 5, 6, 7):
         if q == 6:
             pl.semaphore_wait(relay, 1)
         to = flip(me, q)

time: 39.9 us -> 39.9 us (level)
  no operation moved by 1% of the time
where the time goes in v8:
time: 39.9 us; the launch traced here: 39.8 us
  Pallas kernels  39 us (98%)
  between operations  0.8 us (2%)
    pallas_call x1, Pallas kernels, local_stack(): pl.pallas_call(kernel, out_shape=(out, out, jax.ShapeDtypeStruct((LAYERS...  37.3 us
    pallas_call x1, Pallas kernels, local_stack(): pl.pallas_call(last_layers, out_shape=(jax.ShapeDtypeStruct(x.shape, F32)...  1.68 us

profile of v8, /device:TPU:0, one launch (start us, length us, event | category | flops | bytes accessed | tf_op | source)
XLA Modules:
  0.0 39.8 jit_solution(16360128348803091707)
XLA Ops:
  0.6 37.3 %shard_map.59 = (f32[4,2,128,256]{3,2,1,0:T(8,128)S(1)}, f32[4,2,128,256]{3,2,1,0:T(8,128)S(1)}, bf16[2,8,128,256]{3,2,1,0:T(8,128)(2,1)S(1)}, bf16[2,512,256]{2,1,0:T(8,128)(2,1)S(1)}) custom-call(bf16[4,2,128,256]{3,2,1,0:T(8,128)(2,1)} %bitcast.7, bf16[10,768,512]{2,1,0:T(8,128)(2,1)} %bitcast.6, bf16[10,256,256]{2,1,0:T(8,128)(2,1)} %wres_hbm.1, ...), custom_call_target="tpu_custom_call" | custom-call | tf_op jit(solution)/shard_map/pallas_call | solution.py:366
  37.9 1.7 %shard_map.60 = (f32[8,128,256]{2,1,0:T(8,128)}, f32[8,128,256]{2,1,0:T(8,128)}) custom-call(bf16[2,8,128,256]{3,2,1,0:T(8,128)(2,1)S(1)} %get-tuple-element.6.a_ref, f32[8,128,256]{2,1,0:T(8,128)S(1)} %bitcast.4, f32[8,128,256]{2,1,0:T(8,128)S(1)} %bitcast.5, bf16[2,512,256]{2,1,0:T(8,128)(2,1)S(1)} %get-tuple-element.9.w_ref), custom_call_target="tpu_custom_call" | custom-call | tf_op jit(solution)/shard_map/pallas_call | solution.py:375
